TPU v7x, 512 devices: a whole 4x8x8 slice. The times are simulated.
512 devices in a mesh: seq: 64 (over z_hi, x, y), head: 8 (over z_lo, core).
Axes of the slice: x: 4, y: 8, z: 8 (z_hi: 2, z_lo: 4; z = z_hi * 4 + z_lo), core: 2. Of those that a mesh axis runs over, the one named last changes fastest.
Arguments:
- queries: bfloat16 [12288, 32, 128], P('seq', 'head'), may hold values from -180 to 180
- key_rows: bfloat16 [12288, 8, 128], P('seq', 'head'), may hold values from -4.5 to 4.5
- value_rows: bfloat16 [12288, 8, 128], P('seq', 'head'), may hold values from -24 to 24
- windows: int32 [32], P('head'), may hold values from 768 to 1536, as said below
- sink_counts: int32 [32], P('head'), may hold values from 1 to 4, as said below
- sink_bias: float32 [32], P('head'), may hold values from 3 to 7
- out_weight: bfloat16 [4096, 4096], P('head'), may hold values from -0.09375 to 0.09375
Outputs:
- attn_out: bfloat16 [12288, 4096], P(('seq', 'head'))
Inputs may be any that keep to these rules, and one draw needn't show every extreme that they name: `windows`: each head's window lies between 768 and 1536, and some head has exactly 1536. `sink_counts`: each head has 1 to 4 sink tokens, and some head has exactly 4.
All inputs are finite; a program needn't handle non-finite values.
Results may differ from a plain program's by a relative error of at most 0.018.
Values may be sent and summed in bfloat16 or wider, within the bound.
No kernel may reach another device: no remote copies, remote signals or barrier semaphores. Data moves between devices by JAX's collectives and lax.ppermute only.
A program may use at most 64 MiB of HBM per device.

v0:
```python
import jax
import jax.numpy as jnp
from jax import lax
from jax.sharding import Mesh
from jax.sharding import PartitionSpec as P

WINDOW = 1536
SINKS = 4
SEQ = ("seq_0", "seq_1", "seq_2")
SEQ_HEAD = ("seq_0", "seq_1", "seq_2", "head")


def shifted(block, axis, distance):
    devices = range(lax.axis_size(axis))
    route = [(i - distance, i) for i in devices if i - distance in devices]
    return lax.ppermute(block, axis, route)


def broadcast_by_axis(shard, axes, root):
    shard = jnp.where(lax.axis_index(axes) == root, shard, jnp.zeros_like(shard))
    for axis in axes:
        shard = lax.psum(shard, axis)
    return shard


def cut_along(shard, dim, length):
    dims = shard.shape
    blocks = shard.reshape(*dims[:dim], length, dims[dim] // length, *dims[dim + 1 :])
    return jnp.moveaxis(blocks, dim, 0)


def sent_and_summed(shard, axis, dim):
    blocks = cut_along(shard, dim, lax.axis_size(axis))
    arrived = lax.all_to_all(blocks, axis, split_axis=0, concat_axis=0, tiled=True)
    return arrived.astype(jnp.float32).sum(axis=0)


def attend_block(query_block, band_rows, sink_rows, first_pos, windows, sink_counts, sink_bias):
    tok_rows, local_heads, head_width = query_block.shape
    kv_local = band_rows.shape[2]
    group_size = local_heads // kv_local
    band_span = band_rows.shape[1]
    sink_total = sink_rows.shape[1]
    all_keys = jnp.concatenate([sink_rows[0], band_rows[0]], axis=0)
    all_values = jnp.concatenate([sink_rows[1], band_rows[1]], axis=0)
    grouped = query_block.reshape(tok_rows, kv_local, group_size, head_width)
    score_scale = 1.0 / head_width**0.5
    scores = (
        jnp.einsum("tkgd,skd->kgts", grouped, all_keys, preferred_element_type=jnp.float32)
        * score_scale
    )
    query_pos = first_pos + jnp.arange(tok_rows, dtype=jnp.int32)
    band_pos = first_pos + tok_rows - band_span + jnp.arange(band_span, dtype=jnp.int32)
    sink_pos = jnp.arange(sink_total, dtype=jnp.int32)
    key_pos = jnp.concatenate([sink_pos, band_pos])
    is_sink = jnp.concatenate([jnp.ones((sink_total,), bool), jnp.zeros((band_span,), bool)])
    head_window = windows.reshape(kv_local, group_size, 1, 1)
    head_sinks = sink_counts.reshape(kv_local, group_size, 1, 1)
    head_bias = sink_bias.reshape(kv_local, group_size, 1, 1)
    distance = query_pos[:, None] - key_pos[None, :]
    visible = (distance >= 0) & jnp.where(
        is_sink, key_pos < head_sinks, (distance < head_window) & (key_pos >= head_sinks)
    )
    scores = scores + jnp.where(is_sink, head_bias, 0.0)
    masked = jnp.where(visible, scores, -1e30)
    highest = jnp.max(masked, axis=-1, keepdims=True)
    weights = jnp.where(visible, jnp.exp(masked - highest), 0.0)
    normed = (weights / jnp.sum(weights, axis=-1, keepdims=True)).astype(jnp.bfloat16)
    mixed = jnp.einsum("kgts,skd->tkgd", normed, all_values, preferred_element_type=jnp.float32)
    return mixed.astype(jnp.bfloat16).reshape(tok_rows, local_heads * head_width)


def shards(queries, key_rows, value_rows, windows, sink_counts, sink_bias, out_weight):
    tok_rows = queries.shape[0]
    stacked = jnp.stack([key_rows, value_rows])
    halo_depth = (WINDOW - 1) // tok_rows + 1
    received = [shifted(stacked, SEQ, halo_depth - number) for number in range(halo_depth)]
    halo_rows = jnp.concatenate(received, axis=1)
    band_all = jnp.concatenate([halo_rows, stacked], axis=1)
    sink_rows = broadcast_by_axis(stacked[:, :SINKS], SEQ, 0)
    first_pos = lax.axis_index(SEQ) * tok_rows
    attended = attend_block(
        queries, band_all, sink_rows, first_pos, windows, sink_counts, sink_bias
    )
    mine = sent_and_summed(
        jnp.dot(attended, out_weight, preferred_element_type=jnp.float32).astype(jnp.bfloat16),
        "head",
        0,
    )
    return mine.astype(jnp.bfloat16)


def solution(mesh):
    split = Mesh(
        mesh.devices.reshape(2, 4, 8, mesh.shape["head"]), ("seq_0", "seq_1", "seq_2", "head")
    )
    return jax.shard_map(
        shards,
        mesh=split,
        in_specs=(
            P(SEQ, "head", None),
            P(SEQ, "head", None),
            P(SEQ, "head", None),
            P("head"),
            P("head"),
            P("head"),
            P("head", None),
        ),
        out_specs=P(SEQ_HEAD, None),
        check_vma=False,
    )
```

profile of v0, /device:TPU:256, one launch (start us, length us, event | category | flops | bytes accessed | tf_op | source)
XLA Modules:
  0.0 160.0 jit_solution(8025812477693680216)
XLA Ops:
  0.0 0.9 pad_maximum_fusion
  0.9 4.5 %collective-permute-start.6 = (bf16[2,192,1,128]{3,1,2,0:T(8,128)(2,1)S(1)}, bf16[2,192,1,128]{3,1,2,0:T(8,128)(2,1)S(1)}, u32[]{:S(2)}, u32[]{:S(2)}) collective-permute-start(bf16[2,192,1,128]{3,1,2,0:T(8,128)(2,1)S(1)} %pad_maximum_fusion), channel_id=1, source_target_pairs={{0,16},{8,24},{16,32},{24,40},{32,48},{40,56},{48,64},{56,72},{64,... | collective-permute-start | bytes 294920 | tf_op jit(solution)/shard_map/ppermute | solution.py:16
  5.4 5.8 %collective-permute-start.5 = (bf16[2,192,1,128]{3,1,2,0:T(8,128)(2,1)S(1)}, bf16[2,192,1,128]{3,1,2,0:T(8,128)(2,1)S(1)}, u32[]{:S(2)}, u32[]{:S(2)}) collective-permute-start(bf16[2,192,1,128]{3,1,2,0:T(8,128)(2,1)S(1)} %pad_maximum_fusion), channel_id=1, source_target_pairs={{0,24},{8,32},{16,40},{24,48},{32,56},{40,64},{48,72},{56,80},{64,... | collective-permute-start | bytes 294920 | tf_op jit(solution)/shard_map/ppermute | solution.py:16
  11.2 3.8 %collective-permute-start.4 = (bf16[2,192,1,128]{3,1,2,0:T(8,128)(2,1)S(1)}, bf16[2,192,1,128]{3,1,2,0:T(8,128)(2,1)S(1)}, u32[]{:S(2)}, u32[]{:S(2)}) collective-permute-start(bf16[2,192,1,128]{3,1,2,0:T(8,128)(2,1)S(1)} %pad_maximum_fusion), channel_id=1, source_target_pairs={{0,32},{8,40},{16,48},{24,56},{32,64},{40,72},{48,80},{56,88},{64,... | collective-permute-start | bytes 294920 | tf_op jit(solution)/shard_map/ppermute | solution.py:16
  15.1 6.0 %collective-permute-start.3 = (bf16[2,192,1,128]{3,1,2,0:T(8,128)(2,1)S(1)}, bf16[2,192,1,128]{3,1,2,0:T(8,128)(2,1)S(1)}, u32[]{:S(2)}, u32[]{:S(2)}) collective-permute-start(bf16[2,192,1,128]{3,1,2,0:T(8,128)(2,1)S(1)} %pad_maximum_fusion), channel_id=1, source_target_pairs={{0,40},{8,48},{16,56},{24,64},{32,72},{40,80},{48,88},{56,96},{64,... | collective-permute-start | bytes 294920 | tf_op jit(solution)/shard_map/ppermute | solution.py:16
  21.1 3.4 %collective-permute-start = (bf16[2,192,1,128]{3,1,2,0:T(8,128)(2,1)S(1)}, bf16[2,192,1,128]{3,1,2,0:T(8,128)(2,1)S(1)}, u32[]{:S(2)}, u32[]{:S(2)}) collective-permute-start(bf16[2,192,1,128]{3,1,2,0:T(8,128)(2,1)S(1)} %pad_maximum_fusion), channel_id=1, source_target_pairs={{0,64},{8,72},{16,80},{24,88},{32,96},{40,104},{48,112},{56,120},{... | collective-permute-start | bytes 294920 | tf_op jit(solution)/shard_map/ppermute | solution.py:16
  24.6 0.1 pad_add_fusion
  24.7 0.3 broadcast_compare_fusion
  25.0 0.2 broadcast_subtract_fusion
  25.1 0.7 fusion.20
  25.8 8.8 %psum.21 = bf16[2,4,1,128]{3,1,2,0:T(4,128)(2,1)S(1)} all-reduce(bf16[2,4,1,128]{3,1,2,0:T(4,128)(2,1)S(1)} %fusion.20), channel_id=1, replica_groups=mesh['seq_0'=2,'seq_1'=4,'seq_2'=8,'head'=8] {'seq_0'}, use_global_device_ids=true, to_apply=%region_0.1 | all-reduce | flops 1024 | bytes 4096 | tf_op jit(solution)/shard_map/psum | solution.py:22
  34.7 9.5 %psum.22 = bf16[2,4,1,128]{3,1,2,0:T(4,128)(2,1)S(1)} all-reduce(bf16[2,4,1,128]{3,1,2,0:T(4,128)(2,1)S(1)} %psum.21), channel_id=1, replica_groups=mesh['seq_0'=2,'seq_1'=4,'seq_2'=8,'head'=8] {'seq_1'}, use_global_device_ids=true, to_apply=%region_1.2 | all-reduce | flops 1024 | bytes 4096 | tf_op jit(solution)/shard_map/psum | solution.py:22
  44.1 16.7 %psum.23 = bf16[2,4,1,128]{3,1,2,0:T(4,128)(2,1)S(1)} all-reduce(bf16[2,4,1,128]{3,1,2,0:T(4,128)(2,1)S(1)} %psum.22), channel_id=1, replica_groups=mesh['seq_0'=2,'seq_1'=4,'seq_2'=8,'head'=8] {'seq_2'}, use_global_device_ids=true, to_apply=%region_2.3 | all-reduce | flops 1024 | bytes 4096 | tf_op jit(solution)/shard_map/psum | solution.py:22
  60.8 0.7 broadcast_compare_fusion.2
  61.6 0.8 broadcast_select_fusion
  62.4 3.9 %collective-permute-start.1 = (bf16[2,192,1,128]{3,1,2,0:T(8,128)(2,1)S(1)}, bf16[2,192,1,128]{3,1,2,0:T(8,128)(2,1)S(1)}, u32[]{:S(2)}, u32[]{:S(2)}) collective-permute-start(bf16[2,192,1,128]{3,1,2,0:T(8,128)(2,1)S(1)} %pad_maximum_fusion), channel_id=1, source_target_pairs={{0,56},{8,64},{16,72},{24,80},{32,88},{40,96},{48,104},{56,112},{6... | collective-permute-start | bytes 294920 | tf_op jit(solution)/shard_map/ppermute | solution.py:16
  66.3 9.5 %collective-permute-done.1 = bf16[2,192,1,128]{3,1,2,0:T(8,128)(2,1)S(1)} collective-permute-done((bf16[2,192,1,128]{3,1,2,0:T(8,128)(2,1)S(1)}, bf16[2,192,1,128]{3,1,2,0:T(8,128)(2,1)S(1)}, u32[]{:S(2)}, u32[]{:S(2)}) %collective-permute-start.1) | collective-permute-done | bytes 98336 | tf_op jit(solution)/shard_map/ppermute | solution.py:16
  75.8 3.3 %collective-permute-start.2 = (bf16[2,192,1,128]{3,1,2,0:T(8,128)(2,1)S(1)}, bf16[2,192,1,128]{3,1,2,0:T(8,128)(2,1)S(1)}, u32[]{:S(2)}, u32[]{:S(2)}) collective-permute-start(bf16[2,192,1,128]{3,1,2,0:T(8,128)(2,1)S(1)} %pad_maximum_fusion), channel_id=1, source_target_pairs={{0,48},{8,56},{16,64},{24,72},{32,80},{40,88},{48,96},{56,104},{64... | collective-permute-start | bytes 294920 | tf_op jit(solution)/shard_map/ppermute | solution.py:16
  79.2 10.9 %collective-permute-done.2 = bf16[2,192,1,128]{3,1,2,0:T(8,128)(2,1)S(1)} collective-permute-done((bf16[2,192,1,128]{3,1,2,0:T(8,128)(2,1)S(1)}, bf16[2,192,1,128]{3,1,2,0:T(8,128)(2,1)S(1)}, u32[]{:S(2)}, u32[]{:S(2)}) %collective-permute-start.2) | collective-permute-done | bytes 98336 | tf_op jit(solution)/shard_map/ppermute | solution.py:16
  90.1 5.0 %collective-permute-start.7 = (bf16[2,192,1,128]{3,1,2,0:T(8,128)(2,1)S(1)}, bf16[2,192,1,128]{3,1,2,0:T(8,128)(2,1)S(1)}, u32[]{:S(2)}, u32[]{:S(2)}) collective-permute-start(bf16[2,192,1,128]{3,1,2,0:T(8,128)(2,1)S(1)} %pad_maximum_fusion), channel_id=1, source_target_pairs={{0,8},{8,16},{16,24},{24,32},{32,40},{40,48},{48,56},{56,64},{64,7... | collective-permute-start | bytes 294920 | tf_op jit(solution)/shard_map/ppermute | solution.py:16
  95.2 0.0 collective-permute-done.5
  95.2 0.0 collective-permute-done.6
  95.2 9.5 %collective-permute-done.7 = bf16[2,192,1,128]{3,1,2,0:T(8,128)(2,1)S(1)} collective-permute-done((bf16[2,192,1,128]{3,1,2,0:T(8,128)(2,1)S(1)}, bf16[2,192,1,128]{3,1,2,0:T(8,128)(2,1)S(1)}, u32[]{:S(2)}, u32[]{:S(2)}) %collective-permute-start.7) | collective-permute-done | bytes 98336 | tf_op jit(solution)/shard_map/ppermute | solution.py:16
  104.7 0.8 constant_dynamic-update-slice_fusion
  105.6 0.1 slice_bitcast_fusion.1
  105.7 2.3 %fusion.1 = (f32[4,192]{1,0:T(4,128)S(1)}, f32[1732,192,4]{0,1,2:T(8,128)S(1)}) fusion(f32[4,1732]{1,0:T(4,128)S(1)} %broadcast_select_fusion, s32[192,1732]{1,0:T(8,128)S(1)} %broadcast_subtract_fusion, s32[4]{0:T(128)S(1)} %copy-done.3, pred[4,1732]{1,0:T(4,128)(4,1)S(1)} %get-tuple-element.8, pred[4,1732]{1,0:T(4,128)(4,1)S(1)} %get-tuple-element.7, ...), kind=kOutput, calls=%fused_computation.6 | convolution fusion | flops 352052480 | bytes 7669812 | tf_op jit(solution)/shard_map/tkgd,skd->kgts/dot_general | solution.py:49
  108.0 3.5 %fusion.4 = f32[4,192]{1,0:T(4,128)S(1)} fusion(f32[4,192]{1,0:T(4,128)S(1)} %get-tuple-element.11, f32[4,1732]{1,0:T(4,128)S(1)} %broadcast_select_fusion, f32[1732,192,4]{0,1,2:T(8,128)S(1)} %get-tuple-element.12, pred[4,1732]{1,0:T(4,128)(4,1)S(1)} %get-tuple-element.8, s32[4]{0:T(128)S(1)} %copy-done.3, s32[192,1732]{1,0:T(8,128)S(1)} %broadcast_subtract_fusion, ...), kind=kLoop, calls=%fused_computation.9 | loop fusion | flops 13300992 | bytes 7032884 | tf_op jit(solution)/shard_map/reduce_sum | solution.py:68
  111.5 2.8 %fusion.8 = bf16[192,1,4,128]{3,0,2,1:T(8,128)(2,1)S(1)} fusion(f32[4,192]{1,0:T(4,128)S(1)} %fusion.4, f32[4,192]{1,0:T(4,128)S(1)} %get-tuple-element.11, f32[4,1732]{1,0:T(4,128)S(1)} %broadcast_select_fusion, f32[1732,192,4]{0,1,2:T(8,128)S(1)} %get-tuple-element.12, pred[4,1732]{1,0:T(4,128)(4,1)S(1)} %get-tuple-element.8, s32[4]{0:T(128)S(1)} %copy-done.3, ...), kind=kOutput, calls=%fused_computation.11 | convolution fusion | flops 356142080 | bytes 7672884 | tf_op jit(solution)/shard_map/kgts,skd->tkgd/dot_general | solution.py:69
  114.4 0.2 copy.10
  114.5 1.0 convolution_convert_fusion
  115.5 43.5 %all_to_all.5 = bf16[8,24,4096]{2,1,0:T(8,128)(2,1)S(1)} all-to-all(bf16[8,24,4096]{2,1,0:T(8,128)(2,1)S(1)} %bitcast.58), channel_id=1, replica_groups=mesh['seq_0'=2,'seq_1'=4,'seq_2'=8,'head'=8] {'head'}, dimensions={0} | all-to-all | bytes 3145728 | tf_op jit(solution)/shard_map/all_to_all | solution.py:34
  159.1 0.9 reduce_sum.22
  (23 shorter events, 0.2 us)
Async XLA Ops:
  0.0 105.7 %copy-start = (bf16[192,4,128]{2,1,0:T(4,128)(2,1)S(1)}, bf16[192,4,128]{2,1,0:T(4,128)(2,1)}, u32[]{:S(2)}) copy-start(bf16[192,4,128]{2,1,0:T(4,128)(2,1)} %param.7) | copy-start | bytes 589828
  0.0 105.7 %copy-start.2 = (pred[1732]{0:T(1024)(128)(4,1)S(1)}, pred[1732]{0:T(1024)(128)(4,1)}, u32[]{:S(2)}) copy-start(pred[1732]{0:T(1024)(128)(4,1)} %constant.37.clone.1) | copy-start | bytes 5200
  0.0 105.7 %copy-start.3 = (s32[4]{0:T(128)S(1)}, s32[4]{0:T(128)}, u32[]{:S(2)}) copy-start(s32[4]{0:T(128)} %param.10) | copy-start | bytes 52
  0.9 94.3 %collective-permute-start.6 = (bf16[2,192,1,128]{3,1,2,0:T(8,128)(2,1)S(1)}, bf16[2,192,1,128]{3,1,2,0:T(8,128)(2,1)S(1)}, u32[]{:S(2)}, u32[]{:S(2)}) collective-permute-start(bf16[2,192,1,128]{3,1,2,0:T(8,128)(2,1)S(1)} %pad_maximum_fusion), channel_id=1, source_target_pairs={{0,16},{8,24},{16,32},{24,40},{32,48},{40,56},{48,64},{56,72},{64,... | collective-permute-start | bytes 294920 | tf_op jit(solution)/shard_map/ppermute | solution.py:16
  5.4 89.8 %collective-permute-start.5 = (bf16[2,192,1,128]{3,1,2,0:T(8,128)(2,1)S(1)}, bf16[2,192,1,128]{3,1,2,0:T(8,128)(2,1)S(1)}, u32[]{:S(2)}, u32[]{:S(2)}) collective-permute-start(bf16[2,192,1,128]{3,1,2,0:T(8,128)(2,1)S(1)} %pad_maximum_fusion), channel_id=1, source_target_pairs={{0,24},{8,32},{16,40},{24,48},{32,56},{40,64},{48,72},{56,80},{64,... | collective-permute-start | bytes 294920 | tf_op jit(solution)/shard_map/ppermute | solution.py:16
  11.2 83.9 %collective-permute-start.4 = (bf16[2,192,1,128]{3,1,2,0:T(8,128)(2,1)S(1)}, bf16[2,192,1,128]{3,1,2,0:T(8,128)(2,1)S(1)}, u32[]{:S(2)}, u32[]{:S(2)}) collective-permute-start(bf16[2,192,1,128]{3,1,2,0:T(8,128)(2,1)S(1)} %pad_maximum_fusion), channel_id=1, source_target_pairs={{0,32},{8,40},{16,48},{24,56},{32,64},{40,72},{48,80},{56,88},{64,... | collective-permute-start | bytes 294920 | tf_op jit(solution)/shard_map/ppermute | solution.py:16
  15.1 80.0 %collective-permute-start.3 = (bf16[2,192,1,128]{3,1,2,0:T(8,128)(2,1)S(1)}, bf16[2,192,1,128]{3,1,2,0:T(8,128)(2,1)S(1)}, u32[]{:S(2)}, u32[]{:S(2)}) collective-permute-start(bf16[2,192,1,128]{3,1,2,0:T(8,128)(2,1)S(1)} %pad_maximum_fusion), channel_id=1, source_target_pairs={{0,40},{8,48},{16,56},{24,64},{32,72},{40,80},{48,88},{56,96},{64,... | collective-permute-start | bytes 294920 | tf_op jit(solution)/shard_map/ppermute | solution.py:16
  21.1 41.2 %collective-permute-start = (bf16[2,192,1,128]{3,1,2,0:T(8,128)(2,1)S(1)}, bf16[2,192,1,128]{3,1,2,0:T(8,128)(2,1)S(1)}, u32[]{:S(2)}, u32[]{:S(2)}) collective-permute-start(bf16[2,192,1,128]{3,1,2,0:T(8,128)(2,1)S(1)} %pad_maximum_fusion), channel_id=1, source_target_pairs={{0,64},{8,72},{16,80},{24,88},{32,96},{40,104},{48,112},{56,120},{... | collective-permute-start | bytes 294920 | tf_op jit(solution)/shard_map/ppermute | solution.py:16
  62.4 13.4 %collective-permute-start.1 = (bf16[2,192,1,128]{3,1,2,0:T(8,128)(2,1)S(1)}, bf16[2,192,1,128]{3,1,2,0:T(8,128)(2,1)S(1)}, u32[]{:S(2)}, u32[]{:S(2)}) collective-permute-start(bf16[2,192,1,128]{3,1,2,0:T(8,128)(2,1)S(1)} %pad_maximum_fusion), channel_id=1, source_target_pairs={{0,56},{8,64},{16,72},{24,80},{32,88},{40,96},{48,104},{56,112},{6... | collective-permute-start | bytes 294920 | tf_op jit(solution)/shard_map/ppermute | solution.py:16
  75.8 14.3 %collective-permute-start.2 = (bf16[2,192,1,128]{3,1,2,0:T(8,128)(2,1)S(1)}, bf16[2,192,1,128]{3,1,2,0:T(8,128)(2,1)S(1)}, u32[]{:S(2)}, u32[]{:S(2)}) collective-permute-start(bf16[2,192,1,128]{3,1,2,0:T(8,128)(2,1)S(1)} %pad_maximum_fusion), channel_id=1, source_target_pairs={{0,48},{8,56},{16,64},{24,72},{32,80},{40,88},{48,96},{56,104},{64... | collective-permute-start | bytes 294920 | tf_op jit(solution)/shard_map/ppermute | solution.py:16
  90.1 14.6 %collective-permute-start.7 = (bf16[2,192,1,128]{3,1,2,0:T(8,128)(2,1)S(1)}, bf16[2,192,1,128]{3,1,2,0:T(8,128)(2,1)S(1)}, u32[]{:S(2)}, u32[]{:S(2)}) collective-permute-start(bf16[2,192,1,128]{3,1,2,0:T(8,128)(2,1)S(1)} %pad_maximum_fusion), channel_id=1, source_target_pairs={{0,8},{8,16},{16,24},{24,32},{32,40},{40,48},{48,56},{56,64},{64,7... | collective-permute-start | bytes 294920 | tf_op jit(solution)/shard_map/ppermute | solution.py:16
  111.5 3.0 %copy-start.1 = (bf16[512,4096]{1,0:T(8,128)(2,1)S(1)}, bf16[512,4096]{1,0:T(8,128)(2,1)}, u32[]{:S(2)}) copy-start(bf16[512,4096]{1,0:T(8,128)(2,1)} %param.13) | copy-start | bytes 12582916
where the time goes:
time: 161 us; the launch traced here: 160 us
  blocking collectives  78.5 us (49%)
  starting transfers between devices  35.8 us (22%)
  waiting for transfers between devices  29.9 us (19%)
  other arithmetic  8.87 us (6%)
  matrix products  6.17 us (4%)
    all_to_all x1, blocking collectives, sent_and_summed(): lax.all_to_all(blocks, axis, split_axis=0, concat_axis=0, tiled=True)  43.5 us
    ppermute x8, starting transfers between devices, shifted(): return lax.ppermute(block, axis, route)  35.8 us
    psum x3, blocking collectives, broadcast_by_axis(): shard = lax.psum(shard, axis)  35 us
    ppermute x8, waiting for transfers between devices, shifted(): return lax.ppermute(block, axis, route)  29.9 us
    reduce_sum x1, other arithmetic, attend_block(): jnp.sum(weights, axis=-1, keepdims=True)  3.48 us
  transfers between devices with their start and end apart: 8, of which 3 were waited for; matrix products, arithmetic and copies ran while one was open for 2% of the time, Pallas kernels for 0%

commit v1 on v0

v1 whole, which is shorter than its diff:
```python
import functools

import jax
import jax.numpy as jnp
from jax import lax
from jax.experimental import pallas as pl
from jax.experimental.pallas import tpu as pltpu
from jax.sharding import Mesh
from jax.sharding import PartitionSpec as P

WINDOW = 1536
SINKS = 4
SEQ = ("zh", "x", "y")
HEAD = ("zl", "core")
LANES = 128
NEG = -1e30
LOG2E = 1.4426950408889634
ALWAYS, NEVER = 1 << 30, -(1 << 30)


def attend_kernel(place, win, cnt, bias, q_ref, halo_ref, near_ref, out_ref, *, tok_rows, row_len):
    heads, rows, width = q_ref.shape[1:]
    first_pos, y, part = place[0], place[1], place[2]
    unit = LOG2E / width**0.5
    halo_len = row_len * tok_rows
    near_len = near_ref.shape[1]
    row = lax.broadcasted_iota(jnp.int32, (rows, 1), 0)
    per = rows // 4
    jump = sum((row >= per * k).astype(jnp.int32) for k in range(1, 4))
    tok = row + jump * per + part * per
    query_pos = first_pos + tok
    row_start = first_pos - y * tok_rows
    number = lax.broadcasted_iota(jnp.int32, (1, halo_len), 1)
    halo_pos = row_start + number - jnp.where(number < y * tok_rows, 0, halo_len)
    near = lax.broadcasted_iota(jnp.int32, (1, near_len), 1)
    is_sink = near >= tok_rows
    near_pos = jnp.where(is_sink, near - tok_rows, first_pos + near)
    keys = halo_ref[:, 0].reshape(halo_len, width)
    values = halo_ref[:, 1].reshape(halo_len, width)
    near_keys, near_values = near_ref[0], near_ref[1]
    transposed = (((1,), (1,)), ((), ()))
    for h in range(heads):
        q = q_ref[part, h]
        lowest = jnp.maximum(query_pos - win[h] + 1, cnt[h])
        far = lax.dot_general(q, keys, transposed, preferred_element_type=jnp.float32)
        far = jnp.where(halo_pos >= lowest, far, NEG)
        close = lax.dot_general(q, near_keys, transposed, preferred_element_type=jnp.float32)
        close = close + jnp.where(is_sink, bias[h] * (width**0.5), 0.0)
        ranked = jnp.where(is_sink, jnp.where(near_pos < cnt[h], ALWAYS, NEVER), near_pos)
        close = jnp.where((near_pos <= query_pos) & (ranked >= lowest), close, NEG)
        top = jnp.maximum(
            jnp.max(far, axis=1, keepdims=True), jnp.max(close, axis=1, keepdims=True)
        )
        far = jnp.exp2((far - top) * unit)
        close = jnp.exp2((close - top) * unit)
        total = jnp.sum(far, axis=1, keepdims=True) + jnp.sum(close, axis=1, keepdims=True)
        mixed = jnp.dot(far.astype(jnp.bfloat16), values, preferred_element_type=jnp.float32)
        mixed += jnp.dot(
            close.astype(jnp.bfloat16), near_values, preferred_element_type=jnp.float32
        )
        out_ref[:, h * width : (h + 1) * width] = (mixed / total).astype(out_ref.dtype)


def attend(place, windows, sink_counts, sink_bias, q, halo, near):
    heads, rows, width = q.shape[1:]
    tok_rows = halo.shape[2]
    row_len = halo.shape[0]
    smem = pl.BlockSpec(memory_space=pltpu.SMEM)
    vmem = pl.BlockSpec(memory_space=pltpu.VMEM)
    span = row_len * tok_rows + near.shape[1]
    return pl.pallas_call(
        functools.partial(attend_kernel, tok_rows=tok_rows, row_len=row_len),
        out_shape=jax.ShapeDtypeStruct((rows, heads * width), jnp.bfloat16),
        in_specs=[smem] * 4 + [vmem] * 3,
        out_specs=vmem,
        cost_estimate=pl.CostEstimate(
            flops=4 * heads * rows * span * width,
            bytes_accessed=halo.size * 2,
            transcendentals=heads * rows * span,
        ),
        name="attend",
    )(place, windows, sink_counts, sink_bias, q, halo, near)


def shards(queries, key_rows, value_rows, windows, sink_counts, sink_bias, out_weight):
    tok_rows, heads, width = queries.shape
    row_len = lax.axis_size("y")
    seq_len = lax.axis_size(SEQ)
    y, core = lax.axis_index("y"), lax.axis_index("core")
    first_pos = lax.axis_index(SEQ) * tok_rows
    stacked = jnp.stack([key_rows[:, 0], value_rows[:, 0]])
    before = lax.ppermute(stacked, SEQ, [(i, i + row_len) for i in range(seq_len - row_len)])
    other_weight = lax.ppermute(out_weight, "core", [(0, 1), (1, 0)])
    sinks = stacked[:, :SINKS]
    sinks = lax.all_to_all(
        jnp.broadcast_to(sinks[None], (row_len, *sinks.shape)), "y", 0, 0, tiled=True
    )[0]
    rows_of = lax.axis_size(("zh", "x"))
    sinks = lax.all_to_all(
        jnp.broadcast_to(sinks[None], (rows_of, *sinks.shape)), ("zh", "x"), 0, 0, tiled=True
    )[0]
    target = lax.broadcasted_iota(jnp.int32, (row_len, 1, 1, 1), 0)
    sent = jnp.where(target > y, stacked[None], before[None])
    halo = lax.all_to_all(sent, "y", 0, 0, tiled=True)
    near = jnp.concatenate(
        [stacked, jnp.pad(sinks, ((0, 0), (0, 64 - SINKS), (0, 0)))], axis=1
    )
    members, cores = lax.axis_size("zl"), lax.axis_size("core")
    own = tok_rows // (members * cores)
    q = queries.reshape(members, cores, own, heads, width)
    q = q.transpose(1, 3, 0, 2, 4).reshape(cores, heads, members * own, width)

    def attended(part):
        place = jnp.stack([first_pos, y, part]).astype(jnp.int32)
        return attend(place, windows, sink_counts, sink_bias, q, halo, near)

    theirs = lax.ppermute(attended(1 - core), "core", [(0, 1), (1, 0)])
    mine = attended(core)
    summed = jnp.dot(mine, out_weight, preferred_element_type=jnp.float32) + jnp.dot(
        theirs, other_weight, preferred_element_type=jnp.float32
    )
    parts = summed.astype(jnp.bfloat16).reshape(members, own, -1)
    arrived = lax.all_to_all(parts, "zl", 0, 0, tiled=True)
    return arrived.astype(jnp.float32).sum(axis=0).astype(jnp.bfloat16)


def solution(mesh):
    split = Mesh(mesh.devices.reshape(2, 4, 8, 4, 2), SEQ + HEAD)
    return jax.shard_map(
        shards,
        mesh=split,
        in_specs=(
            P(SEQ, HEAD, None),
            P(SEQ, HEAD, None),
            P(SEQ, HEAD, None),
            P(HEAD),
            P(HEAD),
            P(HEAD),
            P(HEAD, None),
        ),
        out_specs=P(SEQ + HEAD, None),
        check_vma=False,
    )
```

time: 161 us -> 109 us (0.68)
  the two profiles are of different devices: /device:TPU:256 before, /device:TPU:1 now
where the time goes in v1:
time: 109 us; the launch traced here: 108 us
  starting transfers between devices  32.6 us (30%)
  waiting for transfers between devices  29.8 us (27%)
  blocking collectives  24 us (22%)
  Pallas kernels  7.7 us (7%)
  other arithmetic  6.11 us (6%)
  local copies, waits for them, and re-layouts  4.05 us (4%)
  matrix products  3.93 us (4%)
    all_to_all x1, blocking collectives, shards(): arrived = lax.all_to_all(parts, 'zl', 0, 0, tiled=True)  24 us
    all_to_all x1, waiting for transfers between devices, shards(): halo = lax.all_to_all(sent, 'y', 0, 0, tiled=True)  17.4 us
    all_to_all x1, starting transfers between devices, shards(): lax.all_to_all(jnp.broadcast_to(sinks[None], (rows_of, *sinks.shape)), ('...  10.7 us
    ppermute x1, starting transfers between devices, shards(): other_weight = lax.ppermute(out_weight, 'core', [(0, 1), (1, 0)])  8.74 us
    all_to_all x1, waiting for transfers between devices, shards(): lax.all_to_all(jnp.broadcast_to(sinks[None], (rows_of, *sinks.shape)), ('...  7.96 us
    pallas_call x2, Pallas kernels, attend(): pl.pallas_call(functools.partial(attend_kernel, tok_rows=tok_rows, row_le...  7.7 us
    ppermute x1, starting transfers between devices, shards(): theirs = lax.ppermute(attended(1 - core), 'core', [(0, 1), (1, 0)])  4.84 us
    all_to_all x1, waiting for transfers between devices, shards(): lax.all_to_all(jnp.broadcast_to(sinks[None], (row_len, *sinks.shape)), 'y...  4.38 us
  transfers between devices with their start and end apart: 6, of which 3 were waited for; matrix products, arithmetic and copies ran while one was open for 8% of the time, Pallas kernels for 7%

profile of v1, /device:TPU:1, one launch (start us, length us, event | category | flops | bytes accessed | tf_op | source)
XLA Modules:
  0.0 108.2 jit_solution(11867036011745175963)
XLA Ops:
  0.0 8.7 %collective-permute-start.2 = (bf16[512,4096]{1,0:T(8,128)(2,1)}, bf16[512,4096]{1,0:T(8,128)(2,1)}, u32[]{:S(2)}, u32[]{:S(2)}) collective-permute-start(bf16[512,4096]{1,0:T(8,128)(2,1)} %param.13), channel_id=1, source_target_pairs={{0,1},{1,0},{2,3},{3,2},{4,5},{5,4},{6,7},{7,6},{8,9},{9,8},{10,11... | collective-permute-start | bytes 12582920 | tf_op jit(solution)/shard_map/ppermute | solution.py:93
  8.7 0.7 fusion.3
  9.5 0.6 broadcast_in_dim.42
  10.1 3.3 %all-to-all-start.1 = ((bf16[8,2,4,128]{3,2,1,0:T(4,128)(2,1)}), bf16[8,2,4,128]{3,2,1,0:T(4,128)(2,1)S(1)}, u32[]{:S(2)}, u32[]{:S(2)}) async-start(bf16[8,2,4,128]{3,2,1,0:T(4,128)(2,1)} %broadcast_in_dim.42), calls=%async_computation.1 | async-start | bytes 32768 | tf_op jit(solution)/shard_map/all_to_all | solution.py:95
  13.4 0.8 pad_maximum_fusion
  14.3 1.3 %collective-permute-start = (bf16[2,192,128]{2,1,0:T(8,128)(2,1)S(1)}, bf16[2,192,128]{2,1,0:T(8,128)(2,1)S(1)}, u32[]{:S(2)}, u32[]{:S(2)}) collective-permute-start(bf16[2,192,128]{2,1,0:T(8,128)(2,1)S(1)} %pad_maximum_fusion), channel_id=1, source_target_pairs={{0,64},{8,72},{16,80},{24,88},{32,96},{40,104},{48,112},{56,120},{... | collective-permute-start | bytes 294920 | tf_op jit(solution)/shard_map/ppermute | solution.py:92
  15.6 4.4 %all-to-all-done.1 = bf16[8,2,4,128]{3,2,1,0:T(4,128)(2,1)S(1)} async-done(((bf16[8,2,4,128]{3,2,1,0:T(4,128)(2,1)}), bf16[8,2,4,128]{3,2,1,0:T(4,128)(2,1)S(1)}, u32[]{:S(2)}, u32[]{:S(2)}) %all-to-all-start.1) | async-done | bytes 16416 | tf_op jit(solution)/shard_map/all_to_all | solution.py:95
  20.0 0.6 broadcast_in_dim.44
  20.6 10.7 %all-to-all-start.2 = ((bf16[8,2,4,128]{3,2,1,0:T(4,128)(2,1)}), bf16[8,2,4,128]{3,2,1,0:T(4,128)(2,1)S(1)}, u32[]{:S(2)}, u32[]{:S(2)}) async-start(bf16[8,2,4,128]{3,2,1,0:T(4,128)(2,1)} %broadcast_in_dim.44), calls=%async_computation.2 | async-start | bytes 32768 | tf_op jit(solution)/shard_map/all_to_all | solution.py:99
  31.3 0.0 collective-permute-done
  31.3 1.0 broadcast_select_fusion
  32.3 8.0 %all-to-all-done.2 = bf16[8,2,4,128]{3,2,1,0:T(4,128)(2,1)S(1)} async-done(((bf16[8,2,4,128]{3,2,1,0:T(4,128)(2,1)}), bf16[8,2,4,128]{3,2,1,0:T(4,128)(2,1)S(1)}, u32[]{:S(2)}, u32[]{:S(2)}) %all-to-all-start.2) | async-done | bytes 16416 | tf_op jit(solution)/shard_map/all_to_all | solution.py:99
  40.2 3.7 %all-to-all-start = ((bf16[8,2,192,128]{3,2,1,0:T(8,128)(2,1)}), bf16[8,2,192,128]{3,2,1,0:T(8,128)(2,1)S(1)}, u32[]{:S(2)}, u32[]{:S(2)}) async-start(bf16[8,2,192,128]{3,2,1,0:T(8,128)(2,1)} %broadcast_select_fusion), calls=%async_computation | async-start | bytes 1572864 | tf_op jit(solution)/shard_map/all_to_all | solution.py:104
  44.0 1.6 %copy.8 = bf16[4,2,24,4,128]{4,2,0,3,1:T(8,128)(2,1)} copy(bf16[4,2,24,4,128]{4,3,2,1,0:T(4,128)(2,1)} %bitcast.26) | data formatting | bytes 393216 | tf_op jit(solution)/shard_map/reshape | solution.py:110
  45.6 0.7 pad_add_fusion.2.place
  46.2 1.5 %fusion.2.near_ref = bf16[2,256,128]{2,1,0:T(8,128)(2,1)} fusion(bf16[2,4,128]{2,1,0:T(4,128)(2,1)S(1)} %slice_bitcast_fusion, bf16[1,192,128]{2,1,0:T(8,128)(2,1)} %bitcast.22, bf16[1,192,128]{2,1,0:T(8,128)(2,1)} %bitcast.25), kind=kLoop, calls=%fused_computation.5 | loop fusion | flops 524288 | bytes 231424 | tf_op jit(solution)/shard_map/concatenate | solution.py:105
  47.7 17.4 %all-to-all-done.halo_ref = bf16[8,2,192,128]{3,2,1,0:T(8,128)(2,1)S(1)} async-done(((bf16[8,2,192,128]{3,2,1,0:T(8,128)(2,1)}), bf16[8,2,192,128]{3,2,1,0:T(8,128)(2,1)S(1)}, u32[]{:S(2)}, u32[]{:S(2)}) %all-to-all-start) | async-done | bytes 786464 | tf_op jit(solution)/shard_map/all_to_all | solution.py:104
  65.1 0.0 copy-start.1
  65.1 0.9 copy-done.1
  66.0 3.8 %attend.3 = bf16[96,512]{1,0:T(8,128)(2,1)} custom-call(s32[3]{0:T(128)} %pad_add_fusion.2.place, s32[4]{0:T(128)} %win.3, s32[4]{0:T(128)} %cnt.3, f32[4]{0:T(128)} %bias.3, bf16[2,4,96,128]{3,2,1,0:T(8,128)(2,1)} %bitcast.27, bf16[8,2,192,128]{3,2,1,0:T(8,128)(2,1)} %copy-done.1, bf16[2,256,128]{2,1,0:T(8,128)(2,1)} %fusion.2.near_ref), custom_call_target="tpu_custom_call" | custom-call | flops 352321536 | bytes 786432 | tf_op jit(solution)/shard_map/attend/pallas_call | solution.py:71
  69.9 4.8 %collective-permute-start.1 = (bf16[96,512]{1,0:T(8,128)(2,1)}, bf16[96,512]{1,0:T(8,128)(2,1)S(1)}, u32[]{:S(2)}, u32[]{:S(2)}) collective-permute-start(bf16[96,512]{1,0:T(8,128)(2,1)} %attend.3), channel_id=1, source_target_pairs={{0,1},{1,0},{2,3},{3,2},{4,5},{5,4},{6,7},{7,6},{8,9},{9,8},{10,11... | collective-permute-start | bytes 294920 | tf_op jit(solution)/shard_map/ppermute | solution.py:117
  74.7 0.6 pad_add_fusion.place
  75.3 3.9 %attend.2 = bf16[96,512]{1,0:T(8,128)(2,1)} custom-call(s32[3]{0:T(128)} %pad_add_fusion.place, s32[4]{0:T(128)} %win.3, s32[4]{0:T(128)} %cnt.3, f32[4]{0:T(128)} %bias.3, bf16[2,4,96,128]{3,2,1,0:T(8,128)(2,1)} %bitcast.28, bf16[8,2,192,128]{3,2,1,0:T(8,128)(2,1)} %copy-done.1, bf16[2,256,128]{2,1,0:T(8,128)(2,1)} %fusion.2.near_ref), custom_call_target="tpu_custom_call" | custom-call | flops 352321536 | bytes 786432 | tf_op jit(solution)/shard_map/attend/pallas_call | solution.py:71
  79.2 0.0 copy-start
  79.2 0.0 collective-permute-done.1
  79.2 0.0 collective-permute-done.2
  79.2 3.1 %fusion.4 = f32[96,4096]{1,0:T(8,128)S(1)} fusion(bf16[96,512]{1,0:T(8,128)(2,1)S(1)} %collective-permute-done.1, bf16[512,4096]{1,0:T(8,128)(2,1)} %collective-permute-done.2), kind=kOutput, calls=%fused_computation.16 | convolution fusion | flops 402653184 | bytes 5865472 | tf_op jit(solution)/shard_map/dot_general | solution.py:119
  82.3 0.3 copy-done
  82.6 0.0 copy-done.2
  82.6 0.8 fusion
  83.4 24.0 %all_to_all.20 = bf16[4,24,4096]{2,1,0:T(8,128)(2,1)S(1)} all-to-all(bf16[4,24,4096]{2,1,0:T(8,128)(2,1)S(1)} %bitcast.19), channel_id=1, replica_groups=mesh['zh'=2,'x'=4,'y'=8,'zl'=4,'core'=2] {'zl'}, dimensions={0} | all-to-all | bytes 1572864 | tf_op jit(solution)/shard_map/all_to_all | solution.py:123
  107.4 0.8 reduce_sum.12
  (4 shorter events, 0.0 us)
Async XLA Ops:
  0.0 79.2 %collective-permute-start.2 = (bf16[512,4096]{1,0:T(8,128)(2,1)}, bf16[512,4096]{1,0:T(8,128)(2,1)}, u32[]{:S(2)}, u32[]{:S(2)}) collective-permute-start(bf16[512,4096]{1,0:T(8,128)(2,1)} %param.13), channel_id=1, source_target_pairs={{0,1},{1,0},{2,3},{3,2},{4,5},{5,4},{6,7},{7,6},{8,9},{9,8},{10,11... | collective-permute-start | bytes 12582920 | tf_op jit(solution)/shard_map/ppermute | solution.py:93
  10.1 9.9 %all-to-all-start.1 = ((bf16[8,2,4,128]{3,2,1,0:T(4,128)(2,1)}), bf16[8,2,4,128]{3,2,1,0:T(4,128)(2,1)S(1)}, u32[]{:S(2)}, u32[]{:S(2)}) async-start(bf16[8,2,4,128]{3,2,1,0:T(4,128)(2,1)} %broadcast_in_dim.42), calls=%async_computation.1 | async-start | bytes 32768 | tf_op jit(solution)/shard_map/all_to_all | solution.py:95
  14.3 17.0 %collective-permute-start = (bf16[2,192,128]{2,1,0:T(8,128)(2,1)S(1)}, bf16[2,192,128]{2,1,0:T(8,128)(2,1)S(1)}, u32[]{:S(2)}, u32[]{:S(2)}) collective-permute-start(bf16[2,192,128]{2,1,0:T(8,128)(2,1)S(1)} %pad_maximum_fusion), channel_id=1, source_target_pairs={{0,64},{8,72},{16,80},{24,88},{32,96},{40,104},{48,112},{56,120},{... | collective-permute-start | bytes 294920 | tf_op jit(solution)/shard_map/ppermute | solution.py:92
  20.6 19.7 %all-to-all-start.2 = ((bf16[8,2,4,128]{3,2,1,0:T(4,128)(2,1)}), bf16[8,2,4,128]{3,2,1,0:T(4,128)(2,1)S(1)}, u32[]{:S(2)}, u32[]{:S(2)}) async-start(bf16[8,2,4,128]{3,2,1,0:T(4,128)(2,1)} %broadcast_in_dim.44), calls=%async_computation.2 | async-start | bytes 32768 | tf_op jit(solution)/shard_map/all_to_all | solution.py:99
  40.2 24.9 %all-to-all-start = ((bf16[8,2,192,128]{3,2,1,0:T(8,128)(2,1)}), bf16[8,2,192,128]{3,2,1,0:T(8,128)(2,1)S(1)}, u32[]{:S(2)}, u32[]{:S(2)}) async-start(bf16[8,2,192,128]{3,2,1,0:T(8,128)(2,1)} %broadcast_select_fusion), calls=%async_computation | async-start | bytes 1572864 | tf_op jit(solution)/shard_map/all_to_all | solution.py:104
  65.1 0.9 copy-start.1
  69.9 9.3 %collective-permute-start.1 = (bf16[96,512]{1,0:T(8,128)(2,1)}, bf16[96,512]{1,0:T(8,128)(2,1)S(1)}, u32[]{:S(2)}, u32[]{:S(2)}) collective-permute-start(bf16[96,512]{1,0:T(8,128)(2,1)} %attend.3), channel_id=1, source_target_pairs={{0,1},{1,0},{2,3},{3,2},{4,5},{5,4},{6,7},{7,6},{8,9},{9,8},{10,11... | collective-permute-start | bytes 294920 | tf_op jit(solution)/shard_map/ppermute | solution.py:117
  79.2 3.4 %copy-start = (bf16[512,4096]{1,0:T(8,128)(2,1)S(1)}, bf16[512,4096]{1,0:T(8,128)(2,1)}, u32[]{:S(2)}) copy-start(bf16[512,4096]{1,0:T(8,128)(2,1)} %param.13) | copy-start | bytes 12582916
  79.2 3.4 %copy-start.2 = (bf16[96,512]{1,0:T(8,128)(2,1)S(1)}, bf16[96,512]{1,0:T(8,128)(2,1)}, u32[]{:S(2)}) copy-start(bf16[96,512]{1,0:T(8,128)(2,1)} %attend.2) | copy-start | bytes 294916

commit v2 on v1

--- a/solution.py
+++ b/solution.py
@@ -8,13 +8,12 @@
 from jax.sharding import Mesh
 from jax.sharding import PartitionSpec as P
 
-WINDOW = 1536
 SINKS = 4
 SEQ = ("zh", "x", "y")
 HEAD = ("zl", "core")
-LANES = 128
 NEG = -1e30
 LOG2E = 1.4426950408889634
+SPREAD = (("zh", [(0, 1)]), ("x", [(0, 1)]), ("x", [(0, 2), (1, 3)]))
 ALWAYS, NEVER = 1 << 30, -(1 << 30)
 
 
@@ -78,6 +77,7 @@
             bytes_accessed=halo.size * 2,
             transcendentals=heads * rows * span,
         ),
+        compiler_params=pltpu.CompilerParams(vmem_limit_bytes=16 << 20),
         name="attend",
     )(place, windows, sink_counts, sink_bias, q, halo, near)
 
@@ -92,13 +92,11 @@
     before = lax.ppermute(stacked, SEQ, [(i, i + row_len) for i in range(seq_len - row_len)])
     other_weight = lax.ppermute(out_weight, "core", [(0, 1), (1, 0)])
     sinks = stacked[:, :SINKS]
-    sinks = lax.all_to_all(
-        jnp.broadcast_to(sinks[None], (row_len, *sinks.shape)), "y", 0, 0, tiled=True
-    )[0]
-    rows_of = lax.axis_size(("zh", "x"))
-    sinks = lax.all_to_all(
-        jnp.broadcast_to(sinks[None], (rows_of, *sinks.shape)), ("zh", "x"), 0, 0, tiled=True
-    )[0]
+    sinks = jnp.broadcast_to(sinks[None], (row_len, *sinks.shape))
+    sinks = lax.all_to_all(sinks, "y", 0, 0, tiled=True)[0]
+    sinks = jnp.where(lax.axis_index(("zh", "x")) == 0, sinks, jnp.zeros_like(sinks))
+    for axis, route in SPREAD:
+        sinks = sinks + lax.ppermute(sinks, axis, route)
     target = lax.broadcasted_iota(jnp.int32, (row_len, 1, 1, 1), 0)
     sent = jnp.where(target > y, stacked[None], before[None])
     halo = lax.all_to_all(sent, "y", 0, 0, tiled=True)

time: 109 us -> 96.4 us (0.88)
  the two profiles are of different devices: /device:TPU:1 before, /device:TPU:6 now
where the time goes in v2:
time: 96.4 us; the launch traced here: 95.8 us
  starting transfers between devices  35.1 us (36%)
  blocking collectives  27.2 us (28%)
  waiting for transfers between devices  16.5 us (17%)
  Pallas kernels  5.15 us (5%)
  other arithmetic  4.39 us (5%)
  matrix products  3.83 us (4%)
  local copies, waits for them, and re-layouts  3.54 us (4%)
    all_to_all x1, blocking collectives, shards(): arrived = lax.all_to_all(parts, 'zl', 0, 0, tiled=True)  27.2 us
    ppermute x3, waiting for transfers between devices, shards(): sinks = sinks + lax.ppermute(sinks, axis, route)  12 us
    ppermute x1, starting transfers between devices, shards(): lax.ppermute(stacked, SEQ, [(i, i + row_len) for i in range(seq_len - row...  10.8 us
    all_to_all x1, starting transfers between devices, shards(): sinks = lax.all_to_all(sinks, 'y', 0, 0, tiled=True)[0]  7.1 us
    all_to_all x1, starting transfers between devices, shards(): halo = lax.all_to_all(sent, 'y', 0, 0, tiled=True)  6.98 us
    ppermute x3, starting transfers between devices, shards(): sinks = sinks + lax.ppermute(sinks, axis, route)  6.36 us
    pallas_call x2, Pallas kernels, attend(): pl.pallas_call(functools.partial(attend_kernel, tok_rows=tok_rows, row_le...  5.15 us
    dot_general x1, matrix products, shards(): jnp.dot(theirs, other_weight, preferred_element_type=jnp.float32)  3.03 us
  transfers between devices with their start and end apart: 8, of which 4 were waited for; matrix products, arithmetic and copies ran while one was open for 5% of the time, Pallas kernels for 5%

profile of v2, /device:TPU:6, one launch (start us, length us, event | category | flops | bytes accessed | tf_op | source)
XLA Modules:
  0.0 95.8 jit_solution(12077358088308177667)
XLA Ops:
  0.0 1.9 %collective-permute-start.5 = (bf16[512,4096]{1,0:T(8,128)(2,1)}, bf16[512,4096]{1,0:T(8,128)(2,1)}, u32[]{:S(2)}, u32[]{:S(2)}) collective-permute-start(bf16[512,4096]{1,0:T(8,128)(2,1)} %param.13), channel_id=1, source_target_pairs={{0,1},{1,0},{2,3},{3,2},{4,5},{5,4},{6,7},{7,6},{8,9},{9,8},{10,11... | collective-permute-start | bytes 12582920 | tf_op jit(solution)/shard_map/ppermute | solution.py:93
  1.9 0.7 fusion.3
  2.6 0.6 broadcast_in_dim.38
  3.2 7.1 %all-to-all-start.1 = ((bf16[8,2,4,128]{3,2,1,0:T(4,128)(2,1)}), bf16[8,2,4,128]{3,2,1,0:T(4,128)(2,1)S(1)}, u32[]{:S(2)}, u32[]{:S(2)}) async-start(bf16[8,2,4,128]{3,2,1,0:T(4,128)(2,1)} %broadcast_in_dim.38), calls=%async_computation.1 | async-start | bytes 32768 | tf_op jit(solution)/shard_map/all_to_all | solution.py:96
  10.3 0.8 pad_maximum_fusion
  11.2 10.8 %collective-permute-start = (bf16[2,192,128]{2,1,0:T(8,128)(2,1)S(1)}, bf16[2,192,128]{2,1,0:T(8,128)(2,1)S(1)}, u32[]{:S(2)}, u32[]{:S(2)}) collective-permute-start(bf16[2,192,128]{2,1,0:T(8,128)(2,1)S(1)} %pad_maximum_fusion), channel_id=1, source_target_pairs={{0,64},{8,72},{16,80},{24,88},{32,96},{40,104},{48,112},{56,120},{... | collective-permute-start | bytes 294920 | tf_op jit(solution)/shard_map/ppermute | solution.py:92
  22.0 2.4 %collective-permute-done = bf16[2,192,128]{2,1,0:T(8,128)(2,1)S(1)} collective-permute-done((bf16[2,192,128]{2,1,0:T(8,128)(2,1)S(1)}, bf16[2,192,128]{2,1,0:T(8,128)(2,1)S(1)}, u32[]{:S(2)}, u32[]{:S(2)}) %collective-permute-start) | collective-permute-done | bytes 98336 | tf_op jit(solution)/shard_map/ppermute | solution.py:92
  24.4 1.0 %broadcast_select_fusion = bf16[8,2,192,128]{3,2,1,0:T(8,128)(2,1)} fusion(pred[8]{0:T(512)(128)(4,1)S(1)} %iota_compare_fusion.1, bf16[2,192,128]{2,1,0:T(8,128)(2,1)S(1)} %collective-permute-done, bf16[2,192,128]{2,1,0:T(8,128)(2,1)S(1)} %pad_maximum_fusion), kind=kLoop, calls=%fused_computation.2 | loop fusion | flops 393216 | bytes 983048 | tf_op jit(solution)/shard_map/jit(_where)/select_n | solution.py:101
  25.4 0.0 all-to-all-done.1
  25.4 7.0 %all-to-all-start = ((bf16[8,2,192,128]{3,2,1,0:T(8,128)(2,1)}), bf16[8,2,192,128]{3,2,1,0:T(8,128)(2,1)S(1)}, u32[]{:S(2)}, u32[]{:S(2)}) async-start(bf16[8,2,192,128]{3,2,1,0:T(8,128)(2,1)} %broadcast_select_fusion), calls=%async_computation | async-start | bytes 1572864 | tf_op jit(solution)/shard_map/all_to_all | solution.py:102
  32.4 4.4 %collective-permute-start.1 = (bf16[2,4,128]{2,1,0:T(4,128)(2,1)S(1)}, bf16[2,4,128]{2,1,0:T(4,128)(2,1)S(1)}, u32[]{:S(2)}, u32[]{:S(2)}) collective-permute-start(bf16[2,4,128]{2,1,0:T(4,128)(2,1)S(1)} %fusion.4), channel_id=1, source_target_pairs={{0,256},{1,257},{2,258},{3,259},{4,260},{5,261},{6,262},{7,263},{8... | collective-permute-start | bytes 6152 | tf_op jit(solution)/shard_map/ppermute | solution.py:99
  36.9 1.3 %collective-permute-done.1 = bf16[2,4,128]{2,1,0:T(4,128)(2,1)S(1)} collective-permute-done((bf16[2,4,128]{2,1,0:T(4,128)(2,1)S(1)}, bf16[2,4,128]{2,1,0:T(4,128)(2,1)S(1)}, u32[]{:S(2)}, u32[]{:S(2)}) %collective-permute-start.1) | collective-permute-done | bytes 2080 | tf_op jit(solution)/shard_map/ppermute | solution.py:99
  38.2 0.6 collective-permute-start.2
  38.8 1.3 %collective-permute-start.3 = (bf16[2,4,128]{2,1,0:T(4,128)(2,1)S(1)}, bf16[2,4,128]{2,1,0:T(4,128)(2,1)S(1)}, u32[]{:S(2)}, u32[]{:S(2)}) collective-permute-start(bf16[2,4,128]{2,1,0:T(4,128)(2,1)S(1)} %add.27), channel_id=1, source_target_pairs={{0,128},{64,192},{1,129},{65,193},{2,130},{66,194},{3,131},{67,195... | collective-permute-start | bytes 6152 | tf_op jit(solution)/shard_map/ppermute | solution.py:99
  40.1 0.1 pad_add_fusion.2.place
  40.2 1.0 copy.8
  41.2 10.7 %collective-permute-done.3 = bf16[2,4,128]{2,1,0:T(4,128)(2,1)S(1)} collective-permute-done((bf16[2,4,128]{2,1,0:T(4,128)(2,1)S(1)}, bf16[2,4,128]{2,1,0:T(4,128)(2,1)S(1)}, u32[]{:S(2)}, u32[]{:S(2)}) %collective-permute-start.3) | collective-permute-done | bytes 2080 | tf_op jit(solution)/shard_map/ppermute | solution.py:99
  51.9 0.8 fusion.2.near_ref
  52.7 2.1 %all-to-all-done.halo_ref = bf16[8,2,192,128]{3,2,1,0:T(8,128)(2,1)S(1)} async-done(((bf16[8,2,192,128]{3,2,1,0:T(8,128)(2,1)}), bf16[8,2,192,128]{3,2,1,0:T(8,128)(2,1)S(1)}, u32[]{:S(2)}, u32[]{:S(2)}) %all-to-all-start) | async-done | bytes 786464 | tf_op jit(solution)/shard_map/all_to_all | solution.py:102
  54.8 0.7 copy-done
  55.4 0.7 copy-done.1
  56.1 0.7 copy-done.2
  56.8 2.6 %attend.3 = bf16[96,512]{1,0:T(8,128)(2,1)S(1)} custom-call(s32[3]{0:T(128)S(1)} %pad_add_fusion.2.place, s32[4]{0:T(128)S(1)} %copy-done, s32[4]{0:T(128)S(1)} %copy-done.1, f32[4]{0:T(128)S(1)} %copy-done.2, bf16[2,4,96,128]{3,2,1,0:T(8,128)(2,1)S(1)} %bitcast.19, bf16[8,2,192,128]{3,2,1,0:T(8,128)(2,1)S(1)} %all-to-all-done.halo_ref, ...), custom_call_target="tpu_custom_call" | custom-call | flops 352321536 | bytes 786432 | tf_op jit(solution)/shard_map/attend/pallas_call | solution.py:70
  59.3 1.9 %collective-permute-start.4 = (bf16[96,512]{1,0:T(8,128)(2,1)S(1)}, bf16[96,512]{1,0:T(8,128)(2,1)S(1)}, u32[]{:S(2)}, u32[]{:S(2)}) collective-permute-start(bf16[96,512]{1,0:T(8,128)(2,1)S(1)} %attend.3), channel_id=1, source_target_pairs={{0,1},{1,0},{2,3},{3,2},{4,5},{5,4},{6,7},{7,6},{8,9},{9,8},{10,11... | collective-permute-start | bytes 294920 | tf_op jit(solution)/shard_map/ppermute | solution.py:115
  61.3 0.1 pad_add_fusion.place
  61.3 2.6 %attend.2 = bf16[96,512]{1,0:T(8,128)(2,1)S(1)} custom-call(s32[3]{0:T(128)S(1)} %pad_add_fusion.place, s32[4]{0:T(128)S(1)} %copy-done, s32[4]{0:T(128)S(1)} %copy-done.1, f32[4]{0:T(128)S(1)} %copy-done.2, bf16[2,4,96,128]{3,2,1,0:T(8,128)(2,1)S(1)} %bitcast.20, bf16[8,2,192,128]{3,2,1,0:T(8,128)(2,1)S(1)} %all-to-all-done.halo_ref, ...), custom_call_target="tpu_custom_call" | custom-call | flops 352321536 | bytes 786432 | tf_op jit(solution)/shard_map/attend/pallas_call | solution.py:70
  63.9 0.0 collective-permute-done.4
  63.9 0.0 collective-permute-done.5
  63.9 3.0 %fusion.5 = f32[96,4096]{1,0:T(8,128)S(1)} fusion(bf16[96,512]{1,0:T(8,128)(2,1)S(1)} %collective-permute-done.4, bf16[512,4096]{1,0:T(8,128)(2,1)} %collective-permute-done.5), kind=kOutput, calls=%fused_computation.16 | convolution fusion | flops 402653184 | bytes 5865472 | tf_op jit(solution)/shard_map/dot_general | solution.py:117
  67.0 0.8 fusion
  67.8 27.2 %all_to_all.15 = bf16[4,24,4096]{2,1,0:T(8,128)(2,1)S(1)} all-to-all(bf16[4,24,4096]{2,1,0:T(8,128)(2,1)S(1)} %bitcast.21), channel_id=1, replica_groups=mesh['zh'=2,'x'=4,'y'=8,'zl'=4,'core'=2] {'zl'}, dimensions={0} | all-to-all | bytes 1572864 | tf_op jit(solution)/shard_map/all_to_all | solution.py:121
  95.0 0.8 reduce_sum.12
  (11 shorter events, 0.0 us)
Async XLA Ops:
  0.0 63.9 %collective-permute-start.5 = (bf16[512,4096]{1,0:T(8,128)(2,1)}, bf16[512,4096]{1,0:T(8,128)(2,1)}, u32[]{:S(2)}, u32[]{:S(2)}) collective-permute-start(bf16[512,4096]{1,0:T(8,128)(2,1)} %param.13), channel_id=1, source_target_pairs={{0,1},{1,0},{2,3},{3,2},{4,5},{5,4},{6,7},{7,6},{8,9},{9,8},{10,11... | collective-permute-start | bytes 12582920 | tf_op jit(solution)/shard_map/ppermute | solution.py:93
  3.2 22.2 %all-to-all-start.1 = ((bf16[8,2,4,128]{3,2,1,0:T(4,128)(2,1)}), bf16[8,2,4,128]{3,2,1,0:T(4,128)(2,1)S(1)}, u32[]{:S(2)}, u32[]{:S(2)}) async-start(bf16[8,2,4,128]{3,2,1,0:T(4,128)(2,1)} %broadcast_in_dim.38), calls=%async_computation.1 | async-start | bytes 32768 | tf_op jit(solution)/shard_map/all_to_all | solution.py:96
  11.2 13.3 %collective-permute-start = (bf16[2,192,128]{2,1,0:T(8,128)(2,1)S(1)}, bf16[2,192,128]{2,1,0:T(8,128)(2,1)S(1)}, u32[]{:S(2)}, u32[]{:S(2)}) collective-permute-start(bf16[2,192,128]{2,1,0:T(8,128)(2,1)S(1)} %pad_maximum_fusion), channel_id=1, source_target_pairs={{0,64},{8,72},{16,80},{24,88},{32,96},{40,104},{48,112},{56,120},{... | collective-permute-start | bytes 294920 | tf_op jit(solution)/shard_map/ppermute | solution.py:92
  25.4 29.3 %all-to-all-start = ((bf16[8,2,192,128]{3,2,1,0:T(8,128)(2,1)}), bf16[8,2,192,128]{3,2,1,0:T(8,128)(2,1)S(1)}, u32[]{:S(2)}, u32[]{:S(2)}) async-start(bf16[8,2,192,128]{3,2,1,0:T(8,128)(2,1)} %broadcast_select_fusion), calls=%async_computation | async-start | bytes 1572864 | tf_op jit(solution)/shard_map/all_to_all | solution.py:102
  32.4 5.7 %collective-permute-start.1 = (bf16[2,4,128]{2,1,0:T(4,128)(2,1)S(1)}, bf16[2,4,128]{2,1,0:T(4,128)(2,1)S(1)}, u32[]{:S(2)}, u32[]{:S(2)}) collective-permute-start(bf16[2,4,128]{2,1,0:T(4,128)(2,1)S(1)} %fusion.4), channel_id=1, source_target_pairs={{0,256},{1,257},{2,258},{3,259},{4,260},{5,261},{6,262},{7,263},{8... | collective-permute-start | bytes 6152 | tf_op jit(solution)/shard_map/ppermute | solution.py:99
  38.2 0.7 collective-permute-start.2
  38.8 13.0 %collective-permute-start.3 = (bf16[2,4,128]{2,1,0:T(4,128)(2,1)S(1)}, bf16[2,4,128]{2,1,0:T(4,128)(2,1)S(1)}, u32[]{:S(2)}, u32[]{:S(2)}) collective-permute-start(bf16[2,4,128]{2,1,0:T(4,128)(2,1)S(1)} %add.27), channel_id=1, source_target_pairs={{0,128},{64,192},{1,129},{65,193},{2,130},{66,194},{3,131},{67,195... | collective-permute-start | bytes 6152 | tf_op jit(solution)/shard_map/ppermute | solution.py:99
  54.8 0.7 copy-start
  55.4 0.7 copy-start.1
  56.1 0.7 copy-start.2
  56.8 10.2 %copy-start.3 = (bf16[512,4096]{1,0:T(8,128)(2,1)S(1)}, bf16[512,4096]{1,0:T(8,128)(2,1)}, u32[]{:S(2)}) copy-start(bf16[512,4096]{1,0:T(8,128)(2,1)} %param.13) | copy-start | bytes 12582916
  59.3 4.6 %collective-permute-start.4 = (bf16[96,512]{1,0:T(8,128)(2,1)S(1)}, bf16[96,512]{1,0:T(8,128)(2,1)S(1)}, u32[]{:S(2)}, u32[]{:S(2)}) collective-permute-start(bf16[96,512]{1,0:T(8,128)(2,1)S(1)} %attend.3), channel_id=1, source_target_pairs={{0,1},{1,0},{2,3},{3,2},{4,5},{5,4},{6,7},{7,6},{8,9},{9,8},{10,11... | collective-permute-start | bytes 294920 | tf_op jit(solution)/shard_map/ppermute | solution.py:115

commit v3 on v2

--- a/solution.py
+++ b/solution.py
@@ -13,13 +13,26 @@
 HEAD = ("zl", "core")
 NEG = -1e30
 LOG2E = 1.4426950408889634
-SPREAD = (("zh", [(0, 1)]), ("x", [(0, 1)]), ("x", [(0, 2), (1, 3)]))
+SPREAD = tuple(
+    (SEQ, [(i, i + step) for i in range(0, 8, 2 * step)]) for step in (4, 2, 1)
+) + (
+    (SEQ, [(i, i + 32) for i in range(8)]),
+    ("x", [(0, 1)]),
+    ("x", [(0, 2), (1, 3)]),
+)
 ALWAYS, NEVER = 1 << 30, -(1 << 30)
 
 
-def attend_kernel(place, win, cnt, bias, q_ref, halo_ref, near_ref, out_ref, *, tok_rows, row_len):
+def attend_kernel(table, bias, q_ref, halo_ref, near_ref, *refs, tok_rows, row_len, number):
+    fetch = None
+    if number == 1:
+        weight_ref, out_ref, held_ref, done = refs
+        fetch = pltpu.make_async_copy(weight_ref, held_ref, done)
+        fetch.start()
+    else:
+        (out_ref,) = refs
     heads, rows, width = q_ref.shape[1:]
-    first_pos, y, part = place[0], place[1], place[2]
+    first_pos, y, part = table[0], table[1], table[2 + number]
     unit = LOG2E / width**0.5
     halo_len = row_len * tok_rows
     near_len = near_ref.shape[1]
@@ -40,12 +53,13 @@
     transposed = (((1,), (1,)), ((), ()))
     for h in range(heads):
         q = q_ref[part, h]
-        lowest = jnp.maximum(query_pos - win[h] + 1, cnt[h])
+        count = table[4 + heads + h]
+        lowest = jnp.maximum(query_pos - table[4 + h] + 1, count)
         far = lax.dot_general(q, keys, transposed, preferred_element_type=jnp.float32)
         far = jnp.where(halo_pos >= lowest, far, NEG)
         close = lax.dot_general(q, near_keys, transposed, preferred_element_type=jnp.float32)
-        close = close + jnp.where(is_sink, bias[h] * (width**0.5), 0.0)
-        ranked = jnp.where(is_sink, jnp.where(near_pos < cnt[h], ALWAYS, NEVER), near_pos)
+        close = close + jnp.where(is_sink, bias[h], 0.0)
+        ranked = jnp.where(is_sink, jnp.where(near_pos < count, ALWAYS, NEVER), near_pos)
         close = jnp.where((near_pos <= query_pos) & (ranked >= lowest), close, NEG)
         top = jnp.maximum(
             jnp.max(far, axis=1, keepdims=True), jnp.max(close, axis=1, keepdims=True)
@@ -58,9 +72,11 @@
             close.astype(jnp.bfloat16), near_values, preferred_element_type=jnp.float32
         )
         out_ref[:, h * width : (h + 1) * width] = (mixed / total).astype(out_ref.dtype)
+    if fetch is not None:
+        fetch.wait()
 
 
-def attend(place, windows, sink_counts, sink_bias, q, halo, near):
+def attend(number, table, sink_bias, q, halo, near, *weights):
     heads, rows, width = q.shape[1:]
     tok_rows = halo.shape[2]
     row_len = halo.shape[0]
@@ -68,10 +84,14 @@
     vmem = pl.BlockSpec(memory_space=pltpu.VMEM)
     span = row_len * tok_rows + near.shape[1]
     return pl.pallas_call(
-        functools.partial(attend_kernel, tok_rows=tok_rows, row_len=row_len),
-        out_shape=jax.ShapeDtypeStruct((rows, heads * width), jnp.bfloat16),
-        in_specs=[smem] * 4 + [vmem] * 3,
-        out_specs=vmem,
+        functools.partial(attend_kernel, tok_rows=tok_rows, row_len=row_len, number=number),
+        out_shape=[jax.ShapeDtypeStruct((rows, heads * width), jnp.bfloat16)]
+        + [jax.ShapeDtypeStruct(w.shape, w.dtype) for w in weights],
+        in_specs=[smem] * 2
+        + [vmem] * 3
+        + [pl.BlockSpec(memory_space=pl.ANY) for _ in weights],
+        out_specs=[vmem] * (1 + len(weights)),
+        scratch_shapes=[pltpu.SemaphoreType.DMA for _ in weights],
         cost_estimate=pl.CostEstimate(
             flops=4 * heads * rows * span * width,
             bytes_accessed=halo.size * 2,
@@ -79,7 +99,7 @@
         ),
         compiler_params=pltpu.CompilerParams(vmem_limit_bytes=16 << 20),
         name="attend",
-    )(place, windows, sink_counts, sink_bias, q, halo, near)
+    )(table, sink_bias, q, halo, near, *weights)
 
 
 def shards(queries, key_rows, value_rows, windows, sink_counts, sink_bias, out_weight):
@@ -91,10 +111,7 @@
     stacked = jnp.stack([key_rows[:, 0], value_rows[:, 0]])
     before = lax.ppermute(stacked, SEQ, [(i, i + row_len) for i in range(seq_len - row_len)])
     other_weight = lax.ppermute(out_weight, "core", [(0, 1), (1, 0)])
-    sinks = stacked[:, :SINKS]
-    sinks = jnp.broadcast_to(sinks[None], (row_len, *sinks.shape))
-    sinks = lax.all_to_all(sinks, "y", 0, 0, tiled=True)[0]
-    sinks = jnp.where(lax.axis_index(("zh", "x")) == 0, sinks, jnp.zeros_like(sinks))
+    sinks = jnp.where(lax.axis_index(SEQ) == 0, stacked[:, :SINKS], 0)
     for axis, route in SPREAD:
         sinks = sinks + lax.ppermute(sinks, axis, route)
     target = lax.broadcasted_iota(jnp.int32, (row_len, 1, 1, 1), 0)
@@ -108,12 +125,13 @@
     q = queries.reshape(members, cores, own, heads, width)
     q = q.transpose(1, 3, 0, 2, 4).reshape(cores, heads, members * own, width)
 
-    def attended(part):
-        place = jnp.stack([first_pos, y, part]).astype(jnp.int32)
-        return attend(place, windows, sink_counts, sink_bias, q, halo, near)
-
-    theirs = lax.ppermute(attended(1 - core), "core", [(0, 1), (1, 0)])
-    mine = attended(core)
+    place = jnp.stack([first_pos, y, 1 - core, core]).astype(jnp.int32)
+    table = jnp.concatenate([place, windows, sink_counts])
+    halo, other_weight = lax.optimization_barrier((halo, other_weight))
+    bias = sink_bias * width**0.5
+    (theirs,) = attend(0, table, bias, q, halo, near)
+    theirs = lax.ppermute(theirs, "core", [(0, 1), (1, 0)])
+    mine, other_weight = attend(1, table, bias, q, halo, near, other_weight)
     summed = jnp.dot(mine, out_weight, preferred_element_type=jnp.float32) + jnp.dot(
         theirs, other_weight, preferred_element_type=jnp.float32
     )

time: 96.4 us -> 92.5 us (0.960)
  the two profiles are of different devices: /device:TPU:6 before, /device:TPU:62 now
where the time goes in v3:
time: 92.5 us; the launch traced here: 91.9 us
  blocking collectives  27 us (29%)
  starting transfers between devices  26.1 us (28%)
  waiting for transfers between devices  23.5 us (25%)
  other arithmetic  6.31 us (7%)
  Pallas kernels  5.31 us (6%)
  local copies, waits for them, and re-layouts  1.71 us (2%)
  matrix products  1.7 us (2%)
    all_to_all x1, blocking collectives, shards(): arrived = lax.all_to_all(parts, 'zl', 0, 0, tiled=True)  27 us
    ppermute x6, waiting for transfers between devices, shards(): sinks = sinks + lax.ppermute(sinks, axis, route)  20.4 us
    ppermute x1, starting transfers between devices, shards(): lax.ppermute(stacked, SEQ, [(i, i + row_len) for i in range(seq_len - row...  10.8 us
    all_to_all x1, starting transfers between devices, shards(): halo = lax.all_to_all(sent, 'y', 0, 0, tiled=True)  6.87 us
    pallas_call x2, Pallas kernels, attend(): pl.pallas_call(functools.partial(attend_kernel, tok_rows=tok_rows, row_le...  5.31 us
    ppermute x6, starting transfers between devices, shards(): sinks = sinks + lax.ppermute(sinks, axis, route)  4.56 us
    ppermute x1, waiting for transfers between devices, shards(): lax.ppermute(stacked, SEQ, [(i, i + row_len) for i in range(seq_len - row...  2.68 us
    ppermute x1, starting transfers between devices, shards(): theirs = lax.ppermute(theirs, 'core', [(0, 1), (1, 0)])  1.92 us
  transfers between devices with their start and end apart: 10, of which 3 were waited for; matrix products, arithmetic and copies ran while one was open for 9% of the time, Pallas kernels for 0%

profile of v3, /device:TPU:62, one launch (start us, length us, event | category | flops | bytes accessed | tf_op | source)
XLA Modules:
  0.0 91.9 jit_solution(6265976280556150445)
XLA Ops:
  0.0 1.9 %collective-permute-start.1 = (bf16[512,4096]{1,0:T(8,128)(2,1)}, bf16[512,4096]{1,0:T(8,128)(2,1)}, u32[]{:S(2)}, u32[]{:S(2)}) collective-permute-start(bf16[512,4096]{1,0:T(8,128)(2,1)} %param.13), channel_id=1, source_target_pairs={{0,1},{1,0},{2,3},{3,2},{4,5},{5,4},{6,7},{7,6},{8,9},{9,8},{10,11... | collective-permute-start | bytes 12582920 | tf_op jit(solution)/shard_map/ppermute | solution.py:113
  1.9 0.8 pad_maximum_fusion
  2.8 10.8 %collective-permute-start = (bf16[2,192,128]{2,1,0:T(8,128)(2,1)S(1)}, bf16[2,192,128]{2,1,0:T(8,128)(2,1)S(1)}, u32[]{:S(2)}, u32[]{:S(2)}) collective-permute-start(bf16[2,192,128]{2,1,0:T(8,128)(2,1)S(1)} %pad_maximum_fusion), channel_id=1, source_target_pairs={{0,64},{8,72},{16,80},{24,88},{32,96},{40,104},{48,112},{56,120},{... | collective-permute-start | bytes 294920 | tf_op jit(solution)/shard_map/ppermute | solution.py:112
  13.6 2.7 %collective-permute-done = bf16[2,192,128]{2,1,0:T(8,128)(2,1)S(1)} collective-permute-done((bf16[2,192,128]{2,1,0:T(8,128)(2,1)S(1)}, bf16[2,192,128]{2,1,0:T(8,128)(2,1)S(1)}, u32[]{:S(2)}, u32[]{:S(2)}) %collective-permute-start) | collective-permute-done | bytes 98336 | tf_op jit(solution)/shard_map/ppermute | solution.py:112
  16.3 1.0 %broadcast_select_fusion = bf16[8,2,192,128]{3,2,1,0:T(8,128)(2,1)} fusion(pred[8]{0:T(512)(128)(4,1)S(1)} %iota_compare_fusion.1, bf16[2,192,128]{2,1,0:T(8,128)(2,1)S(1)} %collective-permute-done, bf16[2,192,128]{2,1,0:T(8,128)(2,1)S(1)} %pad_maximum_fusion), kind=kLoop, calls=%fused_computation.2 | loop fusion | flops 393216 | bytes 983048 | tf_op jit(solution)/shard_map/jit(_where)/select_n | solution.py:118
  17.3 6.9 %all-to-all-start = ((bf16[8,2,192,128]{3,2,1,0:T(8,128)(2,1)}), bf16[8,2,192,128]{3,2,1,0:T(8,128)(2,1)S(1)}, u32[]{:S(2)}, u32[]{:S(2)}) async-start(bf16[8,2,192,128]{3,2,1,0:T(8,128)(2,1)} %broadcast_select_fusion), calls=%async_computation | async-start | bytes 1572864 | tf_op jit(solution)/shard_map/all_to_all | solution.py:119
  24.2 0.7 fusion.4
  24.9 0.6 collective-permute-start.2
  25.5 0.0 collective-permute-done.2
  25.5 0.7 fusion.10
  26.2 0.6 collective-permute-start.3
  26.9 0.0 collective-permute-done.3
  26.9 0.7 fusion.11
  27.6 0.6 collective-permute-start.4
  28.3 0.7 collective-permute-start.5
  29.0 0.7 collective-permute-start.6
  29.7 1.3 %collective-permute-start.7 = (bf16[2,4,128]{2,1,0:T(4,128)(2,1)S(1)}, bf16[2,4,128]{2,1,0:T(4,128)(2,1)S(1)}, u32[]{:S(2)}, u32[]{:S(2)}) collective-permute-start(bf16[2,4,128]{2,1,0:T(4,128)(2,1)S(1)} %add.37), channel_id=1, source_target_pairs={{0,128},{64,192},{1,129},{65,193},{2,130},{66,194},{3,131},{67,195... | collective-permute-start | bytes 6152 | tf_op jit(solution)/shard_map/ppermute | solution.py:116
  31.0 0.7 broadcast_multiply_fusion.bias
  31.7 1.0 %copy.8 = bf16[4,2,24,4,128]{4,2,0,3,1:T(8,128)(2,1)S(1)} copy(bf16[4,2,24,4,128]{4,3,2,1,0:T(4,128)(2,1)} %bitcast.28) | data formatting | bytes 393216 | tf_op jit(solution)/shard_map/reshape | solution.py:125
  32.6 0.8 concatenate.6.table
  33.4 20.4 %collective-permute-done.7 = bf16[2,4,128]{2,1,0:T(4,128)(2,1)S(1)} collective-permute-done((bf16[2,4,128]{2,1,0:T(4,128)(2,1)S(1)}, bf16[2,4,128]{2,1,0:T(4,128)(2,1)S(1)}, u32[]{:S(2)}, u32[]{:S(2)}) %collective-permute-start.7) | collective-permute-done | bytes 2080 | tf_op jit(solution)/shard_map/ppermute | solution.py:116
  53.8 0.8 fusion.2.near_ref
  54.6 0.0 copy-start
  54.6 0.0 collective-permute-done.1.refs_0_
  54.6 2.6 %attend.3 = bf16[96,512]{1,0:T(8,128)(2,1)S(1)} custom-call(s32[12]{0:T(128)S(1)} %concatenate.6.table, f32[4]{0:T(128)S(1)} %broadcast_multiply_fusion.bias, bf16[2,4,96,128]{3,2,1,0:T(8,128)(2,1)S(1)} %bitcast.15, bf16[8,2,192,128]{3,2,1,0:T(8,128)(2,1)S(1)} %all-to-all-done.halo_ref, bf16[2,256,128]{2,1,0:T(8,128)(2,1)S(1)} %fusion.2.near_ref), custom_call_target="tpu_custom_call" | custom-call | flops 352321536 | bytes 786432 | tf_op jit(solution)/shard_map/attend/pallas_call | solution.py:86
  57.2 2.7 %attend.2 = (bf16[96,512]{1,0:T(8,128)(2,1)S(1)}, bf16[512,4096]{1,0:T(8,128)(2,1)S(1)}) custom-call(s32[12]{0:T(128)S(1)} %concatenate.6.table, f32[4]{0:T(128)S(1)} %broadcast_multiply_fusion.bias, bf16[2,4,96,128]{3,2,1,0:T(8,128)(2,1)S(1)} %bitcast.16, bf16[8,2,192,128]{3,2,1,0:T(8,128)(2,1)S(1)} %all-to-all-done.halo_ref, ...), custom_call_target="tpu_custom_call" | custom-call | flops 352321536 | bytes 786432 | tf_op jit(solution)/shard_map/attend/pallas_call | solution.py:86
  60.0 1.9 %collective-permute-start.8 = (bf16[96,512]{1,0:T(8,128)(2,1)S(1)}, bf16[96,512]{1,0:T(8,128)(2,1)S(1)}, u32[]{:S(2)}, u32[]{:S(2)}) collective-permute-start(bf16[96,512]{1,0:T(8,128)(2,1)S(1)} %attend.3), channel_id=1, source_target_pairs={{0,1},{1,0},{2,3},{3,2},{4,5},{5,4},{6,7},{7,6},{8,9},{9,8},{10,11... | collective-permute-start | bytes 294920 | tf_op jit(solution)/shard_map/ppermute | solution.py:133
  61.9 0.8 fusion.5
  62.7 0.5 collective-permute-done.8
  63.1 0.9 fusion
  64.1 27.0 %all_to_all.10 = bf16[4,24,4096]{2,1,0:T(8,128)(2,1)S(1)} all-to-all(bf16[4,24,4096]{2,1,0:T(8,128)(2,1)S(1)} %bitcast.17), channel_id=1, replica_groups=mesh['zh'=2,'x'=4,'y'=8,'zl'=4,'core'=2] {'zl'}, dimensions={0} | all-to-all | bytes 1572864 | tf_op jit(solution)/shard_map/all_to_all | solution.py:139
  91.0 0.8 reduce_sum.12
  (10 shorter events, 0.0 us)
Async XLA Ops:
  0.0 54.6 %collective-permute-start.1 = (bf16[512,4096]{1,0:T(8,128)(2,1)}, bf16[512,4096]{1,0:T(8,128)(2,1)}, u32[]{:S(2)}, u32[]{:S(2)}) collective-permute-start(bf16[512,4096]{1,0:T(8,128)(2,1)} %param.13), channel_id=1, source_target_pairs={{0,1},{1,0},{2,3},{3,2},{4,5},{5,4},{6,7},{7,6},{8,9},{9,8},{10,11... | collective-permute-start | bytes 12582920 | tf_op jit(solution)/shard_map/ppermute | solution.py:113
  2.8 13.5 %collective-permute-start = (bf16[2,192,128]{2,1,0:T(8,128)(2,1)S(1)}, bf16[2,192,128]{2,1,0:T(8,128)(2,1)S(1)}, u32[]{:S(2)}, u32[]{:S(2)}) collective-permute-start(bf16[2,192,128]{2,1,0:T(8,128)(2,1)S(1)} %pad_maximum_fusion), channel_id=1, source_target_pairs={{0,64},{8,72},{16,80},{24,88},{32,96},{40,104},{48,112},{56,120},{... | collective-permute-start | bytes 294920 | tf_op jit(solution)/shard_map/ppermute | solution.py:112
  17.3 37.3 %all-to-all-start = ((bf16[8,2,192,128]{3,2,1,0:T(8,128)(2,1)}), bf16[8,2,192,128]{3,2,1,0:T(8,128)(2,1)S(1)}, u32[]{:S(2)}, u32[]{:S(2)}) async-start(bf16[8,2,192,128]{3,2,1,0:T(8,128)(2,1)} %broadcast_select_fusion), calls=%async_computation | async-start | bytes 1572864 | tf_op jit(solution)/shard_map/all_to_all | solution.py:119
  24.9 0.7 collective-permute-start.2
  26.2 0.7 collective-permute-start.3
  27.6 0.7 collective-permute-start.4
  28.3 0.7 collective-permute-start.5
  29.0 0.7 collective-permute-start.6
  29.7 24.1 %collective-permute-start.7 = (bf16[2,4,128]{2,1,0:T(4,128)(2,1)S(1)}, bf16[2,4,128]{2,1,0:T(4,128)(2,1)S(1)}, u32[]{:S(2)}, u32[]{:S(2)}) collective-permute-start(bf16[2,4,128]{2,1,0:T(4,128)(2,1)S(1)} %add.37), channel_id=1, source_target_pairs={{0,128},{64,192},{1,129},{65,193},{2,130},{66,194},{3,131},{67,195... | collective-permute-start | bytes 6152 | tf_op jit(solution)/shard_map/ppermute | solution.py:116
  54.6 7.3 %copy-start = (bf16[512,4096]{1,0:T(8,128)(2,1)S(1)}, bf16[512,4096]{1,0:T(8,128)(2,1)}, u32[]{:S(2)}) copy-start(bf16[512,4096]{1,0:T(8,128)(2,1)} %param.13) | copy-start | bytes 12582916
  60.0 3.2 %collective-permute-start.8 = (bf16[96,512]{1,0:T(8,128)(2,1)S(1)}, bf16[96,512]{1,0:T(8,128)(2,1)S(1)}, u32[]{:S(2)}, u32[]{:S(2)}) collective-permute-start(bf16[96,512]{1,0:T(8,128)(2,1)S(1)} %attend.3), channel_id=1, source_target_pairs={{0,1},{1,0},{2,3},{3,2},{4,5},{5,4},{6,7},{7,6},{8,9},{9,8},{10,11... | collective-permute-start | bytes 294920 | tf_op jit(solution)/shard_map/ppermute | solution.py:133

commit v4 on v3

--- a/solution.py
+++ b/solution.py
@@ -13,24 +13,18 @@
 HEAD = ("zl", "core")
 NEG = -1e30
 LOG2E = 1.4426950408889634
-SPREAD = tuple(
-    (SEQ, [(i, i + step) for i in range(0, 8, 2 * step)]) for step in (4, 2, 1)
-) + (
-    (SEQ, [(i, i + 32) for i in range(8)]),
-    ("x", [(0, 1)]),
-    ("x", [(0, 2), (1, 3)]),
+SPREAD = (
+    (SEQ, [(0, 32)]),
+    (SEQ, [(i, i + 8) for i in (0, 32)]),
+    (SEQ, [(i, i + j) for i in (0, 32) for i, j in ((i, 24), (i + 8, 8))]),
+    ("y", [(0, 1)]),
+    ("y", [(0, 7), (1, 2)]),
+    ("y", [(7, 5), (0, 6), (1, 3), (2, 4)]),
 )
 ALWAYS, NEVER = 1 << 30, -(1 << 30)
 
 
-def attend_kernel(table, bias, q_ref, halo_ref, near_ref, *refs, tok_rows, row_len, number):
-    fetch = None
-    if number == 1:
-        weight_ref, out_ref, held_ref, done = refs
-        fetch = pltpu.make_async_copy(weight_ref, held_ref, done)
-        fetch.start()
-    else:
-        (out_ref,) = refs
+def attend_kernel(table, bias, q_ref, halo_ref, near_ref, out_ref, *, tok_rows, row_len, number):
     heads, rows, width = q_ref.shape[1:]
     first_pos, y, part = table[0], table[1], table[2 + number]
     unit = LOG2E / width**0.5
@@ -72,11 +66,9 @@
             close.astype(jnp.bfloat16), near_values, preferred_element_type=jnp.float32
         )
         out_ref[:, h * width : (h + 1) * width] = (mixed / total).astype(out_ref.dtype)
-    if fetch is not None:
-        fetch.wait()
 
 
-def attend(number, table, sink_bias, q, halo, near, *weights):
+def attend(number, table, sink_bias, q, halo, near):
     heads, rows, width = q.shape[1:]
     tok_rows = halo.shape[2]
     row_len = halo.shape[0]
@@ -85,21 +77,17 @@
     span = row_len * tok_rows + near.shape[1]
     return pl.pallas_call(
         functools.partial(attend_kernel, tok_rows=tok_rows, row_len=row_len, number=number),
-        out_shape=[jax.ShapeDtypeStruct((rows, heads * width), jnp.bfloat16)]
-        + [jax.ShapeDtypeStruct(w.shape, w.dtype) for w in weights],
-        in_specs=[smem] * 2
-        + [vmem] * 3
-        + [pl.BlockSpec(memory_space=pl.ANY) for _ in weights],
-        out_specs=[vmem] * (1 + len(weights)),
-        scratch_shapes=[pltpu.SemaphoreType.DMA for _ in weights],
+        out_shape=jax.ShapeDtypeStruct((rows, heads * width), jnp.bfloat16),
+        in_specs=[smem] * 2 + [vmem] * 3,
+        out_specs=vmem,
         cost_estimate=pl.CostEstimate(
-            flops=4 * heads * rows * span * width,
+            flops=32 * heads * rows * span * width,
             bytes_accessed=halo.size * 2,
             transcendentals=heads * rows * span,
         ),
         compiler_params=pltpu.CompilerParams(vmem_limit_bytes=16 << 20),
         name="attend",
-    )(table, sink_bias, q, halo, near, *weights)
+    )(table, sink_bias, q, halo, near)
 
 
 def shards(queries, key_rows, value_rows, windows, sink_counts, sink_bias, out_weight):
@@ -110,7 +98,6 @@
     first_pos = lax.axis_index(SEQ) * tok_rows
     stacked = jnp.stack([key_rows[:, 0], value_rows[:, 0]])
     before = lax.ppermute(stacked, SEQ, [(i, i + row_len) for i in range(seq_len - row_len)])
-    other_weight = lax.ppermute(out_weight, "core", [(0, 1), (1, 0)])
     sinks = jnp.where(lax.axis_index(SEQ) == 0, stacked[:, :SINKS], 0)
     for axis, route in SPREAD:
         sinks = sinks + lax.ppermute(sinks, axis, route)
@@ -127,15 +114,18 @@
 
     place = jnp.stack([first_pos, y, 1 - core, core]).astype(jnp.int32)
     table = jnp.concatenate([place, windows, sink_counts])
-    halo, other_weight = lax.optimization_barrier((halo, other_weight))
     bias = sink_bias * width**0.5
-    (theirs,) = attend(0, table, bias, q, halo, near)
+
+    def projected(rows, weight):
+        return jnp.dot(rows, weight, preferred_element_type=jnp.float32).astype(jnp.bfloat16)
+
+    theirs = attend(0, table, bias, q, halo, near)
+    theirs = projected(theirs, out_weight)
     theirs = lax.ppermute(theirs, "core", [(0, 1), (1, 0)])
-    mine, other_weight = attend(1, table, bias, q, halo, near, other_weight)
-    summed = jnp.dot(mine, out_weight, preferred_element_type=jnp.float32) + jnp.dot(
-        theirs, other_weight, preferred_element_type=jnp.float32
-    )
-    parts = summed.astype(jnp.bfloat16).reshape(members, own, -1)
+    mine = attend(1, table, bias, q, halo, near)
+    mine = projected(mine, out_weight)
+    parts = (mine.astype(jnp.float32) + theirs.astype(jnp.float32)).astype(jnp.bfloat16)
+    parts = parts.reshape(members, own, -1)
     arrived = lax.all_to_all(parts, "zl", 0, 0, tiled=True)
     return arrived.astype(jnp.float32).sum(axis=0).astype(jnp.bfloat16)
 

time: 92.5 us -> 89.9 us (0.972)
  the two profiles are of different devices: /device:TPU:62 before, /device:TPU:20 now
where the time goes in v4:
time: 89.9 us; the launch traced here: 89.4 us
  waiting for transfers between devices  30.6 us (34%)
  blocking collectives  26.2 us (29%)
  starting transfers between devices  17.6 us (20%)
  other arithmetic  6.31 us (7%)
  Pallas kernels  5.12 us (6%)
  local copies, waits for them, and re-layouts  1.71 us (2%)
  matrix products  1.6 us (2%)
    ppermute x6, waiting for transfers between devices, shards(): sinks = sinks + lax.ppermute(sinks, axis, route)  27.2 us
    all_to_all x1, blocking collectives, shards(): arrived = lax.all_to_all(parts, 'zl', 0, 0, tiled=True)  26.2 us
    all_to_all x1, starting transfers between devices, shards(): halo = lax.all_to_all(sent, 'y', 0, 0, tiled=True)  7.43 us
    ppermute x6, starting transfers between devices, shards(): sinks = sinks + lax.ppermute(sinks, axis, route)  5.18 us
    pallas_call x2, Pallas kernels, attend(): pl.pallas_call(functools.partial(attend_kernel, tok_rows=tok_rows, row_le...  5.12 us
    ppermute x1, waiting for transfers between devices, shards(): lax.ppermute(stacked, SEQ, [(i, i + row_len) for i in range(seq_len - row...  3.38 us
    ppermute x1, starting transfers between devices, shards(): lax.ppermute(stacked, SEQ, [(i, i + row_len) for i in range(seq_len - row...  3.11 us
    ppermute x1, starting transfers between devices, shards(): theirs = lax.ppermute(theirs, 'core', [(0, 1), (1, 0)])  1.92 us
  transfers between devices with their start and end apart: 9, of which 2 were waited for; matrix products, arithmetic and copies ran while one was open for 6% of the time, Pallas kernels for 3%

profile of v4, /device:TPU:20, one launch (start us, length us, event | category | flops | bytes accessed | tf_op | source)
XLA Modules:
  0.0 89.4 jit_solution(9159587092704542350)
XLA Ops:
  0.0 0.8 pad_maximum_fusion
  0.8 3.1 %collective-permute-start = (bf16[2,192,128]{2,1,0:T(8,128)(2,1)S(1)}, bf16[2,192,128]{2,1,0:T(8,128)(2,1)S(1)}, u32[]{:S(2)}, u32[]{:S(2)}) collective-permute-start(bf16[2,192,128]{2,1,0:T(8,128)(2,1)S(1)} %pad_maximum_fusion), channel_id=1, source_target_pairs={{0,64},{8,72},{16,80},{24,88},{32,96},{40,104},{48,112},{56,120},{... | collective-permute-start | bytes 294920 | tf_op jit(solution)/shard_map/ppermute | solution.py:100
  4.0 3.4 %collective-permute-done = bf16[2,192,128]{2,1,0:T(8,128)(2,1)S(1)} collective-permute-done((bf16[2,192,128]{2,1,0:T(8,128)(2,1)S(1)}, bf16[2,192,128]{2,1,0:T(8,128)(2,1)S(1)}, u32[]{:S(2)}, u32[]{:S(2)}) %collective-permute-start) | collective-permute-done | bytes 98336 | tf_op jit(solution)/shard_map/ppermute | solution.py:100
  7.3 1.0 %broadcast_select_fusion = bf16[8,2,192,128]{3,2,1,0:T(8,128)(2,1)} fusion(pred[8]{0:T(512)(128)(4,1)S(1)} %iota_compare_fusion.1, bf16[2,192,128]{2,1,0:T(8,128)(2,1)S(1)} %collective-permute-done, bf16[2,192,128]{2,1,0:T(8,128)(2,1)S(1)} %pad_maximum_fusion), kind=kLoop, calls=%fused_computation.5 | loop fusion | flops 393216 | bytes 983048 | tf_op jit(solution)/shard_map/jit(_where)/select_n | solution.py:105
  8.4 7.4 %all-to-all-start = ((bf16[8,2,192,128]{3,2,1,0:T(8,128)(2,1)}), bf16[8,2,192,128]{3,2,1,0:T(8,128)(2,1)S(1)}, u32[]{:S(2)}, u32[]{:S(2)}) async-start(bf16[8,2,192,128]{3,2,1,0:T(8,128)(2,1)} %broadcast_select_fusion), calls=%async_computation | async-start | bytes 1572864 | tf_op jit(solution)/shard_map/all_to_all | solution.py:106
  15.8 0.7 fusion.6
  16.5 0.6 collective-permute-start.1
  17.2 0.0 collective-permute-done.1
  17.2 0.7 fusion.11
  17.9 0.6 collective-permute-start.2
  18.5 0.0 collective-permute-done.2
  18.5 0.7 fusion.12
  19.3 0.6 collective-permute-start.3
  19.9 0.7 collective-permute-start.4
  20.6 1.3 %collective-permute-start.5 = (bf16[2,4,128]{2,1,0:T(4,128)(2,1)S(1)}, bf16[2,4,128]{2,1,0:T(4,128)(2,1)S(1)}, u32[]{:S(2)}, u32[]{:S(2)}) collective-permute-start(bf16[2,4,128]{2,1,0:T(4,128)(2,1)S(1)} %add.36), channel_id=1, source_target_pairs={{0,56},{8,16},{1,57},{9,17},{2,58},{10,18},{3,59},{11,19},{4,60},{... | collective-permute-start | bytes 6152 | tf_op jit(solution)/shard_map/ppermute | solution.py:103
  21.9 27.2 %collective-permute-done.5 = bf16[2,4,128]{2,1,0:T(4,128)(2,1)S(1)} collective-permute-done((bf16[2,4,128]{2,1,0:T(4,128)(2,1)S(1)}, bf16[2,4,128]{2,1,0:T(4,128)(2,1)S(1)}, u32[]{:S(2)}, u32[]{:S(2)}) %collective-permute-start.5) | collective-permute-done | bytes 2080 | tf_op jit(solution)/shard_map/ppermute | solution.py:103
  49.1 1.3 %collective-permute-start.6 = (bf16[2,4,128]{2,1,0:T(4,128)(2,1)S(1)}, bf16[2,4,128]{2,1,0:T(4,128)(2,1)S(1)}, u32[]{:S(2)}, u32[]{:S(2)}) collective-permute-start(bf16[2,4,128]{2,1,0:T(4,128)(2,1)S(1)} %add.37), channel_id=1, source_target_pairs={{56,40},{0,48},{8,24},{16,32},{57,41},{1,49},{9,25},{17,33},{58,42... | collective-permute-start | bytes 6152 | tf_op jit(solution)/shard_map/ppermute | solution.py:103
  50.4 0.7 broadcast_multiply_fusion.bias
  51.1 1.0 %copy.8 = bf16[4,2,24,4,128]{4,2,0,3,1:T(8,128)(2,1)S(1)} copy(bf16[4,2,24,4,128]{4,3,2,1,0:T(4,128)(2,1)} %bitcast.28) | data formatting | bytes 393216 | tf_op jit(solution)/shard_map/reshape | solution.py:112
  52.0 0.8 concatenate.6.table
  52.8 0.0 collective-permute-done.6
  52.8 0.8 fusion.4.near_ref
  53.6 0.0 all-to-all-done.halo_ref
  53.6 0.0 copy-start
  53.6 2.6 %attend.3 = bf16[96,512]{1,0:T(8,128)(2,1)S(1)} custom-call(s32[12]{0:T(128)S(1)} %concatenate.6.table, f32[4]{0:T(128)S(1)} %broadcast_multiply_fusion.bias, bf16[2,4,96,128]{3,2,1,0:T(8,128)(2,1)S(1)} %bitcast.15, bf16[8,2,192,128]{3,2,1,0:T(8,128)(2,1)S(1)} %all-to-all-done.halo_ref, bf16[2,256,128]{2,1,0:T(8,128)(2,1)S(1)} %fusion.4.near_ref), custom_call_target="tpu_custom_call" | custom-call | flops 2818572288 | bytes 786432 | tf_op jit(solution)/shard_map/attend/pallas_call | solution.py:78
  56.2 0.8 convolution_convert_fusion
  57.0 1.9 %collective-permute-start.7 = (bf16[96,4096]{1,0:T(8,128)(2,1)S(1)}, bf16[96,4096]{1,0:T(8,128)(2,1)S(1)}, u32[]{:S(2)}, u32[]{:S(2)}) collective-permute-start(bf16[96,4096]{1,0:T(8,128)(2,1)S(1)} %convolution_convert_fusion), channel_id=1, source_target_pairs={{0,1},{1,0},{2,3},{3,2},{4,5},{5,4},{6,7},{7,6},{8,9},{9,8},{10,11... | collective-permute-start | bytes 2359304 | tf_op jit(solution)/shard_map/ppermute | solution.py:124
  58.9 2.6 %attend.2 = bf16[96,512]{1,0:T(8,128)(2,1)S(1)} custom-call(s32[12]{0:T(128)S(1)} %concatenate.6.table, f32[4]{0:T(128)S(1)} %broadcast_multiply_fusion.bias, bf16[2,4,96,128]{3,2,1,0:T(8,128)(2,1)S(1)} %bitcast.16, bf16[8,2,192,128]{3,2,1,0:T(8,128)(2,1)S(1)} %all-to-all-done.halo_ref, bf16[2,256,128]{2,1,0:T(8,128)(2,1)S(1)} %fusion.4.near_ref), custom_call_target="tpu_custom_call" | custom-call | flops 2818572288 | bytes 786432 | tf_op jit(solution)/shard_map/attend/pallas_call | solution.py:78
  61.5 0.0 collective-permute-done.7
  61.5 0.8 fusion.2
  62.3 26.2 %all_to_all.10 = bf16[4,24,4096]{2,1,0:T(8,128)(2,1)S(1)} all-to-all(bf16[4,24,4096]{2,1,0:T(8,128)(2,1)S(1)} %bitcast.17), channel_id=1, replica_groups=mesh['zh'=2,'x'=4,'y'=8,'zl'=4,'core'=2] {'zl'}, dimensions={0} | all-to-all | bytes 1572864 | tf_op jit(solution)/shard_map/all_to_all | solution.py:129
  88.5 0.8 reduce_sum.12
  (8 shorter events, 0.0 us)
Async XLA Ops:
  0.8 6.5 %collective-permute-start = (bf16[2,192,128]{2,1,0:T(8,128)(2,1)S(1)}, bf16[2,192,128]{2,1,0:T(8,128)(2,1)S(1)}, u32[]{:S(2)}, u32[]{:S(2)}) collective-permute-start(bf16[2,192,128]{2,1,0:T(8,128)(2,1)S(1)} %pad_maximum_fusion), channel_id=1, source_target_pairs={{0,64},{8,72},{16,80},{24,88},{32,96},{40,104},{48,112},{56,120},{... | collective-permute-start | bytes 294920 | tf_op jit(solution)/shard_map/ppermute | solution.py:100
  8.4 45.3 %all-to-all-start = ((bf16[8,2,192,128]{3,2,1,0:T(8,128)(2,1)}), bf16[8,2,192,128]{3,2,1,0:T(8,128)(2,1)S(1)}, u32[]{:S(2)}, u32[]{:S(2)}) async-start(bf16[8,2,192,128]{3,2,1,0:T(8,128)(2,1)} %broadcast_select_fusion), calls=%async_computation | async-start | bytes 1572864 | tf_op jit(solution)/shard_map/all_to_all | solution.py:106
  16.5 0.7 collective-permute-start.1
  17.9 0.7 collective-permute-start.2
  19.3 0.7 collective-permute-start.3
  19.9 0.7 collective-permute-start.4
  20.6 28.5 %collective-permute-start.5 = (bf16[2,4,128]{2,1,0:T(4,128)(2,1)S(1)}, bf16[2,4,128]{2,1,0:T(4,128)(2,1)S(1)}, u32[]{:S(2)}, u32[]{:S(2)}) collective-permute-start(bf16[2,4,128]{2,1,0:T(4,128)(2,1)S(1)} %add.36), channel_id=1, source_target_pairs={{0,56},{8,16},{1,57},{9,17},{2,58},{10,18},{3,59},{11,19},{4,60},{... | collective-permute-start | bytes 6152 | tf_op jit(solution)/shard_map/ppermute | solution.py:103
  49.1 3.7 %collective-permute-start.6 = (bf16[2,4,128]{2,1,0:T(4,128)(2,1)S(1)}, bf16[2,4,128]{2,1,0:T(4,128)(2,1)S(1)}, u32[]{:S(2)}, u32[]{:S(2)}) collective-permute-start(bf16[2,4,128]{2,1,0:T(4,128)(2,1)S(1)} %add.37), channel_id=1, source_target_pairs={{56,40},{0,48},{8,24},{16,32},{57,41},{1,49},{9,25},{17,33},{58,42... | collective-permute-start | bytes 6152 | tf_op jit(solution)/shard_map/ppermute | solution.py:103
  53.6 2.6 %copy-start = (bf16[512,4096]{1,0:T(8,128)(2,1)S(1)}, bf16[512,4096]{1,0:T(8,128)(2,1)}, u32[]{:S(2)}) copy-start(bf16[512,4096]{1,0:T(8,128)(2,1)} %param.13) | copy-start | bytes 12582916
  57.0 4.5 %collective-permute-start.7 = (bf16[96,4096]{1,0:T(8,128)(2,1)S(1)}, bf16[96,4096]{1,0:T(8,128)(2,1)S(1)}, u32[]{:S(2)}, u32[]{:S(2)}) collective-permute-start(bf16[96,4096]{1,0:T(8,128)(2,1)S(1)} %convolution_convert_fusion), channel_id=1, source_target_pairs={{0,1},{1,0},{2,3},{3,2},{4,5},{5,4},{6,7},{7,6},{8,9},{9,8},{10,11... | collective-permute-start | bytes 2359304 | tf_op jit(solution)/shard_map/ppermute | solution.py:124

commit v5 on v4

v5 whole, which is shorter than its diff:
```python
import functools

import jax
import jax.numpy as jnp
from jax import lax
from jax.experimental import pallas as pl
from jax.experimental.pallas import tpu as pltpu
from jax.sharding import Mesh
from jax.sharding import PartitionSpec as P

SINKS = 4
SEQ = ("zh", "x", "y")
HEAD = ("zl", "core")
NEG = -1e30
LOG2E = 1.4426950408889634
SPREAD = (
    (SEQ, [(0, 32)]),
    (SEQ, [(i, i + 8) for i in (0, 32)]),
    (SEQ, [(i, i + j) for i in (0, 32) for i, j in ((i, 24), (i + 8, 8))]),
    ("y", [(0, 1)]),
    ("y", [(0, 7), (1, 2)]),
    ("y", [(7, 5), (0, 6), (1, 3), (2, 4)]),
)
ALWAYS, NEVER = 1 << 30, -(1 << 30)


def attend_kernel(
    table, bias, q_ref, halo_ref, near_ref, out_ref, score_ref, prob_ref, *, tok_rows, number
):
    heads, rows, width = q_ref.shape[1:]
    first_pos, y, member, part = table[0], table[1], table[2], table[3 + number]
    unit = LOG2E / width**0.5
    halo_len = halo_ref.shape[0] * tok_rows
    span = score_ref.shape[1]
    per = rows // 4
    row = lax.broadcasted_iota(jnp.int32, (rows, 1), 0)
    turn = sum((row >= per * k).astype(jnp.int32) for k in range(1, 4))
    query_pos = first_pos + (turn ^ member) * (2 * per) + part * per + row - turn * per
    row_start = first_pos - y * tok_rows
    place = lax.broadcasted_iota(jnp.int32, (1, halo_len), 1)
    halo_pos = row_start + place - jnp.where(place < y * tok_rows, 0, halo_len)
    near = lax.broadcasted_iota(jnp.int32, (1, span - halo_len), 1)
    is_sink = near >= tok_rows
    near_pos = jnp.where(is_sink, near - tok_rows, first_pos + near)
    q = q_ref[part].reshape(heads * rows, width)
    transposed = (((1,), (1,)), ((), ()))
    keys = jnp.concatenate([halo_ref[:, 0].reshape(halo_len, width), near_ref[0]], axis=0)
    score_ref[...] = lax.dot_general(q, keys, transposed, preferred_element_type=jnp.float32)
    totals = []
    for h in range(heads):
        count = table[5 + heads + h]
        lowest = jnp.maximum(query_pos - table[5 + h] + 1, count)
        ranked = jnp.where(is_sink, jnp.where(near_pos < count, ALWAYS, NEVER), near_pos)
        mine = slice(h * rows, (h + 1) * rows)
        far = jnp.where(halo_pos >= lowest, score_ref[mine, :halo_len], NEG)
        close = score_ref[mine, halo_len:] + jnp.where(is_sink, bias[h], 0.0)
        close = jnp.where((near_pos <= query_pos) & (ranked >= lowest), close, NEG)
        top = jnp.maximum(
            jnp.max(far, axis=1, keepdims=True), jnp.max(close, axis=1, keepdims=True)
        )
        far = jnp.exp2((far - top) * unit)
        close = jnp.exp2((close - top) * unit)
        totals.append(jnp.sum(far, axis=1, keepdims=True) + jnp.sum(close, axis=1, keepdims=True))
        prob_ref[mine, :halo_len] = far.astype(jnp.bfloat16)
        prob_ref[mine, halo_len:] = close.astype(jnp.bfloat16)
    values = jnp.concatenate([halo_ref[:, 1].reshape(halo_len, width), near_ref[1]], axis=0)
    mixed = jnp.dot(prob_ref[...], values, preferred_element_type=jnp.float32)
    for h in range(heads):
        block = mixed[h * rows : (h + 1) * rows] / totals[h]
        out_ref[:, h * width : (h + 1) * width] = block.astype(out_ref.dtype)


def attend(number, table, sink_bias, q, halo, near):
    heads, rows, width = q.shape[1:]
    tok_rows = halo.shape[2]
    smem = pl.BlockSpec(memory_space=pltpu.SMEM)
    vmem = pl.BlockSpec(memory_space=pltpu.VMEM)
    span = halo.shape[0] * tok_rows + near.shape[1]
    return pl.pallas_call(
        functools.partial(attend_kernel, tok_rows=tok_rows, number=number),
        out_shape=jax.ShapeDtypeStruct((rows, heads * width), jnp.bfloat16),
        in_specs=[smem] * 2 + [vmem] * 3,
        out_specs=vmem,
        scratch_shapes=[
            pltpu.VMEM((heads * rows, span), jnp.float32),
            pltpu.VMEM((heads * rows, span), jnp.bfloat16),
        ],
        cost_estimate=pl.CostEstimate(
            flops=32 * heads * rows * span * width,
            bytes_accessed=halo.size * 2,
            transcendentals=heads * rows * span,
        ),
        compiler_params=pltpu.CompilerParams(vmem_limit_bytes=20 << 20),
        name="attend",
    )(table, sink_bias, q, halo, near)


def project_kernel(rows_ref, weight_ref, theirs_ref, *out_refs):
    per = out_refs[0].shape[0]
    step = 512

    @pl.loop(0, weight_ref.shape[1] // step)
    def _(k):
        columns = pl.ds(pl.multiple_of(k * step, step), step)
        total = jnp.dot(rows_ref[...], weight_ref[:, columns], preferred_element_type=jnp.float32)
        total = total.astype(jnp.bfloat16).astype(jnp.float32)
        total = total + theirs_ref[:, columns].astype(jnp.float32)
        for number, out_ref in enumerate(out_refs):
            out_ref[:, columns] = total[number * per : (number + 1) * per].astype(out_ref.dtype)


def project(rows, weight, theirs, members):
    vmem = pl.BlockSpec(memory_space=pltpu.VMEM)
    per, columns = rows.shape[0] // members, weight.shape[1]
    return pl.pallas_call(
        project_kernel,
        out_shape=[jax.ShapeDtypeStruct((per, columns), jnp.bfloat16)] * members,
        in_specs=[vmem] * 3,
        out_specs=[vmem] * members,
        cost_estimate=pl.CostEstimate(
            flops=2 * rows.size * columns, bytes_accessed=weight.size * 2, transcendentals=0
        ),
        compiler_params=pltpu.CompilerParams(vmem_limit_bytes=20 << 20),
        name="project",
    )(rows, weight, theirs)


def shards(queries, key_rows, value_rows, windows, sink_counts, sink_bias, out_weight):
    tok_rows, heads, width = queries.shape
    row_len = lax.axis_size("y")
    seq_len = lax.axis_size(SEQ)
    y, core = lax.axis_index("y"), lax.axis_index("core")
    first_pos = lax.axis_index(SEQ) * tok_rows
    stacked = jnp.stack([key_rows[:, 0], value_rows[:, 0]])
    before = lax.ppermute(stacked, SEQ, [(i, i + row_len) for i in range(seq_len - row_len)])
    sinks = jnp.where(lax.axis_index(SEQ) == 0, stacked[:, :SINKS], 0)
    for axis, route in SPREAD:
        sinks = sinks + lax.ppermute(sinks, axis, route)
    target = lax.broadcasted_iota(jnp.int32, (row_len, 1, 1, 1), 0)
    sent = jnp.where(target > y, stacked[None], before[None])
    halo = lax.all_to_all(sent, "y", 0, 0, tiled=True)
    near = jnp.concatenate(
        [stacked, jnp.pad(sinks, ((0, 0), (0, 64 - SINKS), (0, 0)))], axis=1
    )
    members, cores = lax.axis_size("zl"), lax.axis_size("core")
    own = tok_rows // (members * cores)
    member = lax.axis_index("zl")
    q = queries.reshape(2, 2, cores, own, heads, width)
    q = jnp.where(member % 2 == 1, jnp.stack([q[:, 1], q[:, 0]], axis=1), q)
    q = jnp.where(member // 2 == 1, jnp.stack([q[1], q[0]]), q)
    q = q.reshape(members, cores, own, heads, width)
    q = q.transpose(1, 3, 0, 2, 4).reshape(cores, heads, members * own, width)
    place = jnp.stack([first_pos, y, member, 1 - core, core]).astype(jnp.int32)
    table = jnp.concatenate([place, windows, sink_counts])
    bias = sink_bias * width**0.5
    theirs = attend(0, table, bias, q, halo, near)
    theirs = jnp.dot(theirs, out_weight, preferred_element_type=jnp.float32).astype(jnp.bfloat16)
    theirs = lax.ppermute(theirs, "core", [(0, 1), (1, 0)])
    mine = attend(1, table, bias, q, halo, near)
    parts = project(mine, out_weight, theirs, members)
    total = parts[0].astype(jnp.float32)
    for distance in (3, 2, 1):
        route = [(i, i ^ distance) for i in range(members)]
        total += lax.ppermute(parts[distance], "zl", route).astype(jnp.float32)
    return total.astype(jnp.bfloat16)


def solution(mesh):
    split = Mesh(mesh.devices.reshape(2, 4, 8, 4, 2), SEQ + HEAD)
    return jax.shard_map(
        shards,
        mesh=split,
        in_specs=(
            P(SEQ, HEAD, None),
            P(SEQ, HEAD, None),
            P(SEQ, HEAD, None),
            P(HEAD),
            P(HEAD),
            P(HEAD),
            P(HEAD, None),
        ),
        out_specs=P(SEQ + HEAD, None),
        check_vma=False,
    )
```

time: 89.9 us -> 82.8 us (0.921)
  the two profiles are of different devices: /device:TPU:20 before, /device:TPU:385 now
where the time goes in v5:
time: 82.8 us; the launch traced here: 82.3 us
  waiting for transfers between devices  38.2 us (46%)
  starting transfers between devices  29.2 us (35%)
  Pallas kernels  6.99 us (8%)
  other arithmetic  5.46 us (7%)
  local copies, waits for them, and re-layouts  1.26 us (2%)
    ppermute x6, waiting for transfers between devices, shards(): sinks = sinks + lax.ppermute(sinks, axis, route)  16.8 us
    ppermute x3, waiting for transfers between devices, shards(): total += lax.ppermute(parts[distance], 'zl', route).astype(jnp.float32)  15.8 us
    ppermute x6, starting transfers between devices, shards(): sinks = sinks + lax.ppermute(sinks, axis, route)  8.52 us
    ppermute x3, starting transfers between devices, shards(): total += lax.ppermute(parts[distance], 'zl', route).astype(jnp.float32)  8.37 us
    all_to_all x1, starting transfers between devices, shards(): halo = lax.all_to_all(sent, 'y', 0, 0, tiled=True)  6.82 us
    pallas_call x2, Pallas kernels, attend(): pl.pallas_call(functools.partial(attend_kernel, tok_rows=tok_rows, number...  5.17 us
    all_to_all x1, waiting for transfers between devices, shards(): halo = lax.all_to_all(sent, 'y', 0, 0, tiled=True)  4.98 us
    ppermute x1, starting transfers between devices, shards(): lax.ppermute(stacked, SEQ, [(i, i + row_len) for i in range(seq_len - row...  3.12 us
  transfers between devices with their start and end apart: 12, of which 9 were waited for; matrix products, arithmetic and copies ran while one was open for 6% of the time, Pallas kernels for 3%

profile of v5, /device:TPU:385, one launch (start us, length us, event | category | flops | bytes accessed | tf_op | source)
XLA Modules:
  0.0 82.3 jit_solution(8689721064797276475)
XLA Ops:
  0.0 0.9 %pad_maximum_fusion.2 = bf16[2,192,128]{2,1,0:T(8,128)(2,1)S(1)} fusion(bf16[1,192,128]{2,1,0:T(8,128)(2,1)} %bitcast.21, bf16[1,192,128]{2,1,0:T(8,128)(2,1)} %bitcast.26), kind=kLoop, calls=%fused_computation.12 | loop fusion | flops 49152 | bytes 196608 | tf_op jit(solution)/shard_map/stack | solution.py:134
  0.9 3.1 %collective-permute-start = (bf16[2,192,128]{2,1,0:T(8,128)(2,1)S(1)}, bf16[2,192,128]{2,1,0:T(8,128)(2,1)S(1)}, u32[]{:S(2)}, u32[]{:S(2)}) collective-permute-start(bf16[2,192,128]{2,1,0:T(8,128)(2,1)S(1)} %pad_maximum_fusion.2), channel_id=1, source_target_pairs={{0,64},{8,72},{16,80},{24,88},{32,96},{40,104},{48,112},{56,120},{... | collective-permute-start | bytes 294920 | tf_op jit(solution)/shard_map/ppermute | solution.py:135
  4.1 0.7 fusion.4
  4.8 1.3 %collective-permute-start.1 = (bf16[2,4,128]{2,1,0:T(4,128)(2,1)S(1)}, bf16[2,4,128]{2,1,0:T(4,128)(2,1)S(1)}, u32[]{:S(2)}, u32[]{:S(2)}) collective-permute-start(bf16[2,4,128]{2,1,0:T(4,128)(2,1)S(1)} %fusion.4), channel_id=1, source_target_pairs={{0,256},{1,257},{2,258},{3,259},{4,260},{5,261},{6,262},{7,263}} | collective-permute-start | bytes 6152 | tf_op jit(solution)/shard_map/ppermute | solution.py:138
  6.1 1.0 %fusion.6 = (bf16[2,1,2,24,4,128]{5,4,3,2,1,0:T(4,128)(2,1)S(1)}, bf16[2,1,2,24,4,128]{5,4,3,2,1,0:T(4,128)(2,1)S(1)}) fusion(bf16[2,2,2,24,4,128]{5,4,3,2,1,0:T(4,128)(2,1)} %bitcast.18), kind=kLoop, calls=%fused_computation.19 | loop fusion | bytes 393216 | tf_op jit(solution)/shard_map/slice | solution.py:149
  7.1 5.9 %collective-permute-done.1 = bf16[2,4,128]{2,1,0:T(4,128)(2,1)S(1)} collective-permute-done((bf16[2,4,128]{2,1,0:T(4,128)(2,1)S(1)}, bf16[2,4,128]{2,1,0:T(4,128)(2,1)S(1)}, u32[]{:S(2)}, u32[]{:S(2)}) %collective-permute-start.1) | collective-permute-done | bytes 2080 | tf_op jit(solution)/shard_map/ppermute | solution.py:138
  13.0 0.7 fusion.9
  13.7 1.3 %collective-permute-start.2 = (bf16[2,4,128]{2,1,0:T(4,128)(2,1)S(1)}, bf16[2,4,128]{2,1,0:T(4,128)(2,1)S(1)}, u32[]{:S(2)}, u32[]{:S(2)}) collective-permute-start(bf16[2,4,128]{2,1,0:T(4,128)(2,1)S(1)} %fusion.9), channel_id=1, source_target_pairs={{0,64},{256,320},{1,65},{257,321},{2,66},{258,322},{3,67},{259,323... | collective-permute-start | bytes 6152 | tf_op jit(solution)/shard_map/ppermute | solution.py:138
  15.0 0.6 collective-permute-done
  15.6 1.0 %broadcast_select_fusion = bf16[8,2,192,128]{3,2,1,0:T(8,128)(2,1)} fusion(pred[8]{0:T(512)(128)(4,1)S(1)} %iota_compare_fusion.1, bf16[2,192,128]{2,1,0:T(8,128)(2,1)S(1)} %collective-permute-done, bf16[2,192,128]{2,1,0:T(8,128)(2,1)S(1)} %pad_maximum_fusion.2), kind=kLoop, calls=%fused_computation.1 | loop fusion | flops 393216 | bytes 983048 | tf_op jit(solution)/shard_map/jit(_where)/select_n | solution.py:140
  16.7 6.8 %all-to-all-start = ((bf16[8,2,192,128]{3,2,1,0:T(8,128)(2,1)}), bf16[8,2,192,128]{3,2,1,0:T(8,128)(2,1)S(1)}, u32[]{:S(2)}, u32[]{:S(2)}) async-start(bf16[8,2,192,128]{3,2,1,0:T(8,128)(2,1)} %broadcast_select_fusion), calls=%async_computation | async-start | bytes 1572864 | tf_op jit(solution)/shard_map/all_to_all | solution.py:141
  23.5 1.1 %pad_maximum_fusion = (bf16[2,2,2,24,4,128]{5,4,3,2,1,0:T(4,128)(2,1)S(1)}, bf16[2,2,2,24,4,128]{5,4,3,2,1,0:T(4,128)(2,1)S(1)}) fusion(bf16[2,1,2,24,4,128]{5,4,3,2,1,0:T(4,128)(2,1)S(1)} %get-tuple-element.18, bf16[2,1,2,24,4,128]{5,4,3,2,1,0:T(4,128)(2,1)S(1)} %get-tuple-element.17, bf16[2,2,2,24,4,128]{5,4,3,2,1,0:T(4,128)(2,1)} %bitcast.19, pred[]{:T(512)S(6)} %eq.12), kind=kLoop, calls=%fused_computation.5 | loop fusion | flops 196608 | bytes 786433 | tf_op jit(solution)/shard_map/stack | solution.py:149
  24.7 1.3 %collective-permute-start.3 = (bf16[2,4,128]{2,1,0:T(4,128)(2,1)S(1)}, bf16[2,4,128]{2,1,0:T(4,128)(2,1)S(1)}, u32[]{:S(2)}, u32[]{:S(2)}) collective-permute-start(bf16[2,4,128]{2,1,0:T(4,128)(2,1)S(1)} %fusion.10), channel_id=1, source_target_pairs={{0,192},{64,128},{256,448},{320,384},{1,193},{65,129},{257,449},{3... | collective-permute-start | bytes 6152 | tf_op jit(solution)/shard_map/ppermute | solution.py:138
  26.0 0.6 collective-permute-done.3
  26.7 2.1 %collective-permute-start.4 = (bf16[2,4,128]{2,1,0:T(4,128)(2,1)S(1)}, bf16[2,4,128]{2,1,0:T(4,128)(2,1)S(1)}, u32[]{:S(2)}, u32[]{:S(2)}) collective-permute-start(bf16[2,4,128]{2,1,0:T(4,128)(2,1)S(1)} %add.47), channel_id=1, source_target_pairs={{0,8},{1,9},{2,10},{3,11},{4,12},{5,13},{6,14},{7,15},{64,72},{65,... | collective-permute-start | bytes 6152 | tf_op jit(solution)/shard_map/ppermute | solution.py:138
  29.0 9.0 %collective-permute-done.4 = bf16[2,4,128]{2,1,0:T(4,128)(2,1)S(1)} collective-permute-done((bf16[2,4,128]{2,1,0:T(4,128)(2,1)S(1)}, bf16[2,4,128]{2,1,0:T(4,128)(2,1)S(1)}, u32[]{:S(2)}, u32[]{:S(2)}) %collective-permute-start.4) | collective-permute-done | bytes 2080 | tf_op jit(solution)/shard_map/ppermute | solution.py:138
  38.0 1.3 %collective-permute-start.5 = (bf16[2,4,128]{2,1,0:T(4,128)(2,1)S(1)}, bf16[2,4,128]{2,1,0:T(4,128)(2,1)S(1)}, u32[]{:S(2)}, u32[]{:S(2)}) collective-permute-start(bf16[2,4,128]{2,1,0:T(4,128)(2,1)S(1)} %add.48), channel_id=1, source_target_pairs={{0,56},{8,16},{1,57},{9,17},{2,58},{10,18},{3,59},{11,19},{4,60},{... | collective-permute-start | bytes 6152 | tf_op jit(solution)/shard_map/ppermute | solution.py:138
  39.4 0.7 collective-permute-done.5
  40.0 1.3 %collective-permute-start.6 = (bf16[2,4,128]{2,1,0:T(4,128)(2,1)S(1)}, bf16[2,4,128]{2,1,0:T(4,128)(2,1)S(1)}, u32[]{:S(2)}, u32[]{:S(2)}) collective-permute-start(bf16[2,4,128]{2,1,0:T(4,128)(2,1)S(1)} %add.49), channel_id=1, source_target_pairs={{56,40},{0,48},{8,24},{16,32},{57,41},{1,49},{9,25},{17,33},{58,42... | collective-permute-start | bytes 6152 | tf_op jit(solution)/shard_map/ppermute | solution.py:138
  41.5 0.6 collective-permute-done.6
  42.1 5.0 %all-to-all-done.halo_ref = bf16[8,2,192,128]{3,2,1,0:T(8,128)(2,1)S(1)} async-done(((bf16[8,2,192,128]{3,2,1,0:T(8,128)(2,1)}), bf16[8,2,192,128]{3,2,1,0:T(8,128)(2,1)S(1)}, u32[]{:S(2)}, u32[]{:S(2)}) %all-to-all-start) | async-done | bytes 786464 | tf_op jit(solution)/shard_map/all_to_all | solution.py:141
  47.1 2.6 %attend.3 = bf16[96,512]{1,0:T(8,128)(2,1)S(1)} custom-call(s32[13]{0:T(128)S(1)} %concatenate.6.table, f32[4]{0:T(128)S(1)} %broadcast_multiply_fusion.bias, bf16[2,4,96,128]{3,2,1,0:T(8,128)(2,1)S(1)} %bitcast.16, bf16[8,2,192,128]{3,2,1,0:T(8,128)(2,1)S(1)} %all-to-all-done.halo_ref, bf16[2,256,128]{2,1,0:T(8,128)(2,1)S(1)} %fusion.2.near_ref), custom_call_target="tpu_custom_call" | custom-call | flops 2818572288 | bytes 786432 | tf_op jit(solution)/shard_map/attend/pallas_call | solution.py:79
  49.7 0.8 convolution_convert_fusion
  50.5 2.4 %collective-permute-start.7 = (bf16[96,4096]{1,0:T(8,128)(2,1)S(1)}, bf16[96,4096]{1,0:T(8,128)(2,1)S(1)}, u32[]{:S(2)}, u32[]{:S(2)}) collective-permute-start(bf16[96,4096]{1,0:T(8,128)(2,1)S(1)} %convolution_convert_fusion), channel_id=1, source_target_pairs={{0,1},{1,0},{2,3},{3,2},{4,5},{5,4},{6,7},{7,6},{8,9},{9,8},{10,11... | collective-permute-start | bytes 2359304 | tf_op jit(solution)/shard_map/ppermute | solution.py:158
  52.9 2.6 %attend.2.rows_ref = bf16[96,512]{1,0:T(8,128)(2,1)S(1)} custom-call(s32[13]{0:T(128)S(1)} %concatenate.6.table, f32[4]{0:T(128)S(1)} %broadcast_multiply_fusion.bias, bf16[2,4,96,128]{3,2,1,0:T(8,128)(2,1)S(1)} %bitcast.17, bf16[8,2,192,128]{3,2,1,0:T(8,128)(2,1)S(1)} %all-to-all-done.halo_ref, bf16[2,256,128]{2,1,0:T(8,128)(2,1)S(1)} %fusion.2.near_ref), custom_call_target="tpu_custom_call" | custom-call | flops 2818572288 | bytes 786432 | tf_op jit(solution)/shard_map/attend/pallas_call | solution.py:79
  55.5 1.8 %project.1 = (bf16[24,4096]{1,0:T(8,128)(2,1)S(1)}, bf16[24,4096]{1,0:T(8,128)(2,1)S(1)}, bf16[24,4096]{1,0:T(8,128)(2,1)S(1)}, bf16[24,4096]{1,0:T(8,128)(2,1)S(1)}) custom-call(bf16[96,512]{1,0:T(8,128)(2,1)S(1)} %attend.2.rows_ref, bf16[512,4096]{1,0:T(8,128)(2,1)S(1)} %copy-done, bf16[96,4096]{1,0:T(8,128)(2,1)S(1)} %collective-permute-done.7.theirs_ref), custom_call_target="tpu_custom_call" | custom-call | flops 402653184 | bytes 4194304 | tf_op jit(solution)/shard_map/project/pallas_call | solution.py:115
  57.3 1.9 %collective-permute-start.10 = (bf16[24,4096]{1,0:T(8,128)(2,1)S(1)}, bf16[24,4096]{1,0:T(8,128)(2,1)S(1)}, u32[]{:S(2)}, u32[]{:S(2)}) collective-permute-start(bf16[24,4096]{1,0:T(8,128)(2,1)S(1)} %get-tuple-element.12), channel_id=1, source_target_pairs={{0,2},{2,0},{4,6},{6,4},{1,3},{3,1},{5,7},{7,5},{8,10},{10,8},{12,... | collective-permute-start | bytes 589832 | tf_op jit(solution)/shard_map/ppermute | solution.py:164
  59.2 1.9 %collective-permute-start.9 = (bf16[24,4096]{1,0:T(8,128)(2,1)S(1)}, bf16[24,4096]{1,0:T(8,128)(2,1)S(1)}, u32[]{:S(2)}, u32[]{:S(2)}) collective-permute-start(bf16[24,4096]{1,0:T(8,128)(2,1)S(1)} %get-tuple-element.11), channel_id=1, source_target_pairs={{0,4},{2,6},{4,0},{6,2},{1,5},{3,7},{5,1},{7,3},{8,12},{10,14},{12... | collective-permute-start | bytes 589832 | tf_op jit(solution)/shard_map/ppermute | solution.py:164
  61.1 4.5 %collective-permute-start.8 = (bf16[24,4096]{1,0:T(8,128)(2,1)S(1)}, bf16[24,4096]{1,0:T(8,128)(2,1)S(1)}, u32[]{:S(2)}, u32[]{:S(2)}) collective-permute-start(bf16[24,4096]{1,0:T(8,128)(2,1)S(1)} %get-tuple-element.10), channel_id=1, source_target_pairs={{0,6},{2,4},{4,2},{6,0},{1,7},{3,5},{5,3},{7,1},{8,14},{10,12},{12... | collective-permute-start | bytes 589832 | tf_op jit(solution)/shard_map/ppermute | solution.py:164
  65.7 8.2 %collective-permute-done.9 = bf16[24,4096]{1,0:T(8,128)(2,1)S(1)} collective-permute-done((bf16[24,4096]{1,0:T(8,128)(2,1)S(1)}, bf16[24,4096]{1,0:T(8,128)(2,1)S(1)}, u32[]{:S(2)}, u32[]{:S(2)}) %collective-permute-start.9) | collective-permute-done | bytes 196640 | tf_op jit(solution)/shard_map/ppermute | solution.py:164
  73.9 7.6 %collective-permute-done.8 = bf16[24,4096]{1,0:T(8,128)(2,1)S(1)} collective-permute-done((bf16[24,4096]{1,0:T(8,128)(2,1)S(1)}, bf16[24,4096]{1,0:T(8,128)(2,1)S(1)}, u32[]{:S(2)}, u32[]{:S(2)}) %collective-permute-start.8) | collective-permute-done | bytes 196640 | tf_op jit(solution)/shard_map/ppermute | solution.py:164
  81.5 0.8 add_convert_fusion
  (31 shorter events, 0.5 us)
Async XLA Ops:
  0.0 24.6 %copy-start.2 = (bf16[192,1,128]{2,0,1:T(8,128)(2,1)S(1)}, bf16[192,1,128]{2,0,1:T(8,128)(2,1)}, u32[]{:S(2)}) copy-start(bf16[192,1,128]{2,0,1:T(8,128)(2,1)} %param.9) | copy-start | bytes 147460
  0.0 24.6 %copy-start.3 = (bf16[192,1,128]{2,0,1:T(8,128)(2,1)S(1)}, bf16[192,1,128]{2,0,1:T(8,128)(2,1)}, u32[]{:S(2)}) copy-start(bf16[192,1,128]{2,0,1:T(8,128)(2,1)} %param.8) | copy-start | bytes 147460
  0.0 39.3 %copy-start.1 = (bf16[192,4,128]{2,1,0:T(4,128)(2,1)S(1)}, bf16[192,4,128]{2,1,0:T(4,128)(2,1)}, u32[]{:S(2)}) copy-start(bf16[192,4,128]{2,1,0:T(4,128)(2,1)} %param.7) | copy-start | bytes 589828
  0.0 41.3 %copy-start.6 = (f32[4]{0:T(128)S(1)}, f32[4]{0:T(128)}, u32[]{:S(2)}) copy-start(f32[4]{0:T(128)} %param.12) | copy-start | bytes 52
  0.0 41.3 %copy-start.4 = (s32[4]{0:T(128)S(1)}, s32[4]{0:T(128)}, u32[]{:S(2)}) copy-start(s32[4]{0:T(128)} %param.10) | copy-start | bytes 52
  0.0 41.3 %copy-start.5 = (s32[4]{0:T(128)S(1)}, s32[4]{0:T(128)}, u32[]{:S(2)}) copy-start(s32[4]{0:T(128)} %param.11) | copy-start | bytes 52
  0.9 14.7 %collective-permute-start = (bf16[2,192,128]{2,1,0:T(8,128)(2,1)S(1)}, bf16[2,192,128]{2,1,0:T(8,128)(2,1)S(1)}, u32[]{:S(2)}, u32[]{:S(2)}) collective-permute-start(bf16[2,192,128]{2,1,0:T(8,128)(2,1)S(1)} %pad_maximum_fusion.2), channel_id=1, source_target_pairs={{0,64},{8,72},{16,80},{24,88},{32,96},{40,104},{48,112},{56,120},{... | collective-permute-start | bytes 294920 | tf_op jit(solution)/shard_map/ppermute | solution.py:135
  4.8 8.2 %collective-permute-start.1 = (bf16[2,4,128]{2,1,0:T(4,128)(2,1)S(1)}, bf16[2,4,128]{2,1,0:T(4,128)(2,1)S(1)}, u32[]{:S(2)}, u32[]{:S(2)}) collective-permute-start(bf16[2,4,128]{2,1,0:T(4,128)(2,1)S(1)} %fusion.4), channel_id=1, source_target_pairs={{0,256},{1,257},{2,258},{3,259},{4,260},{5,261},{6,262},{7,263}} | collective-permute-start | bytes 6152 | tf_op jit(solution)/shard_map/ppermute | solution.py:138
  13.7 10.9 %collective-permute-start.2 = (bf16[2,4,128]{2,1,0:T(4,128)(2,1)S(1)}, bf16[2,4,128]{2,1,0:T(4,128)(2,1)S(1)}, u32[]{:S(2)}, u32[]{:S(2)}) collective-permute-start(bf16[2,4,128]{2,1,0:T(4,128)(2,1)S(1)} %fusion.9), channel_id=1, source_target_pairs={{0,64},{256,320},{1,65},{257,321},{2,66},{258,322},{3,67},{259,323... | collective-permute-start | bytes 6152 | tf_op jit(solution)/shard_map/ppermute | solution.py:138
  16.7 30.4 %all-to-all-start = ((bf16[8,2,192,128]{3,2,1,0:T(8,128)(2,1)}), bf16[8,2,192,128]{3,2,1,0:T(8,128)(2,1)S(1)}, u32[]{:S(2)}, u32[]{:S(2)}) async-start(bf16[8,2,192,128]{3,2,1,0:T(8,128)(2,1)} %broadcast_select_fusion), calls=%async_computation | async-start | bytes 1572864 | tf_op jit(solution)/shard_map/all_to_all | solution.py:141
  24.7 2.0 %collective-permute-start.3 = (bf16[2,4,128]{2,1,0:T(4,128)(2,1)S(1)}, bf16[2,4,128]{2,1,0:T(4,128)(2,1)S(1)}, u32[]{:S(2)}, u32[]{:S(2)}) collective-permute-start(bf16[2,4,128]{2,1,0:T(4,128)(2,1)S(1)} %fusion.10), channel_id=1, source_target_pairs={{0,192},{64,128},{256,448},{320,384},{1,193},{65,129},{257,449},{3... | collective-permute-start | bytes 6152 | tf_op jit(solution)/shard_map/ppermute | solution.py:138
  26.7 11.3 %collective-permute-start.4 = (bf16[2,4,128]{2,1,0:T(4,128)(2,1)S(1)}, bf16[2,4,128]{2,1,0:T(4,128)(2,1)S(1)}, u32[]{:S(2)}, u32[]{:S(2)}) collective-permute-start(bf16[2,4,128]{2,1,0:T(4,128)(2,1)S(1)} %add.47), channel_id=1, source_target_pairs={{0,8},{1,9},{2,10},{3,11},{4,12},{5,13},{6,14},{7,15},{64,72},{65,... | collective-permute-start | bytes 6152 | tf_op jit(solution)/shard_map/ppermute | solution.py:138
  38.0 2.0 %collective-permute-start.5 = (bf16[2,4,128]{2,1,0:T(4,128)(2,1)S(1)}, bf16[2,4,128]{2,1,0:T(4,128)(2,1)S(1)}, u32[]{:S(2)}, u32[]{:S(2)}) collective-permute-start(bf16[2,4,128]{2,1,0:T(4,128)(2,1)S(1)} %add.48), channel_id=1, source_target_pairs={{0,56},{8,16},{1,57},{9,17},{2,58},{10,18},{3,59},{11,19},{4,60},{... | collective-permute-start | bytes 6152 | tf_op jit(solution)/shard_map/ppermute | solution.py:138
  40.0 2.0 %collective-permute-start.6 = (bf16[2,4,128]{2,1,0:T(4,128)(2,1)S(1)}, bf16[2,4,128]{2,1,0:T(4,128)(2,1)S(1)}, u32[]{:S(2)}, u32[]{:S(2)}) collective-permute-start(bf16[2,4,128]{2,1,0:T(4,128)(2,1)S(1)} %add.49), channel_id=1, source_target_pairs={{56,40},{0,48},{8,24},{16,32},{57,41},{1,49},{9,25},{17,33},{58,42... | collective-permute-start | bytes 6152 | tf_op jit(solution)/shard_map/ppermute | solution.py:138
  47.0 2.6 %copy-start = (bf16[512,4096]{1,0:T(8,128)(2,1)S(1)}, bf16[512,4096]{1,0:T(8,128)(2,1)}, u32[]{:S(2)}) copy-start(bf16[512,4096]{1,0:T(8,128)(2,1)} %weight_ref.1) | copy-start | bytes 12582916
  50.5 5.0 %collective-permute-start.7 = (bf16[96,4096]{1,0:T(8,128)(2,1)S(1)}, bf16[96,4096]{1,0:T(8,128)(2,1)S(1)}, u32[]{:S(2)}, u32[]{:S(2)}) collective-permute-start(bf16[96,4096]{1,0:T(8,128)(2,1)S(1)} %convolution_convert_fusion), channel_id=1, source_target_pairs={{0,1},{1,0},{2,3},{3,2},{4,5},{5,4},{6,7},{7,6},{8,9},{9,8},{10,11... | collective-permute-start | bytes 2359304 | tf_op jit(solution)/shard_map/ppermute | solution.py:158
  57.3 8.4 %collective-permute-start.10 = (bf16[24,4096]{1,0:T(8,128)(2,1)S(1)}, bf16[24,4096]{1,0:T(8,128)(2,1)S(1)}, u32[]{:S(2)}, u32[]{:S(2)}) collective-permute-start(bf16[24,4096]{1,0:T(8,128)(2,1)S(1)} %get-tuple-element.12), channel_id=1, source_target_pairs={{0,2},{2,0},{4,6},{6,4},{1,3},{3,1},{5,7},{7,5},{8,10},{10,8},{12,... | collective-permute-start | bytes 589832 | tf_op jit(solution)/shard_map/ppermute | solution.py:164
  59.2 14.7 %collective-permute-start.9 = (bf16[24,4096]{1,0:T(8,128)(2,1)S(1)}, bf16[24,4096]{1,0:T(8,128)(2,1)S(1)}, u32[]{:S(2)}, u32[]{:S(2)}) collective-permute-start(bf16[24,4096]{1,0:T(8,128)(2,1)S(1)} %get-tuple-element.11), channel_id=1, source_target_pairs={{0,4},{2,6},{4,0},{6,2},{1,5},{3,7},{5,1},{7,3},{8,12},{10,14},{12... | collective-permute-start | bytes 589832 | tf_op jit(solution)/shard_map/ppermute | solution.py:164
  61.1 20.4 %collective-permute-start.8 = (bf16[24,4096]{1,0:T(8,128)(2,1)S(1)}, bf16[24,4096]{1,0:T(8,128)(2,1)S(1)}, u32[]{:S(2)}, u32[]{:S(2)}) collective-permute-start(bf16[24,4096]{1,0:T(8,128)(2,1)S(1)} %get-tuple-element.10), channel_id=1, source_target_pairs={{0,6},{2,4},{4,2},{6,0},{1,7},{3,5},{5,3},{7,1},{8,14},{10,12},{12... | collective-permute-start | bytes 589832 | tf_op jit(solution)/shard_map/ppermute | solution.py:164
